TPU v7x, 8 devices: a whole 2x2x1 slice. The times are simulated.
8 devices in a mesh: sp: 8 (over z, y, x, core).
Axes of the slice: x: 2, y: 2, z: 1, core: 2. Of those that a mesh axis runs over, the one named last changes fastest.
Arguments:
- x: bfloat16 [32, 1024, 2048], P(None, 'sp')
- dy: bfloat16 [32, 1024, 2048], P(None, 'sp')
- prefix_len: int32 [32], replicated
- w_norm: bfloat16 [2048], replicated
- w_q: bfloat16 [2048, 2048], replicated
- w_k: bfloat16 [2048, 128], replicated
- w_v: bfloat16 [2048, 128], replicated
- w_o: bfloat16 [2048, 2048], replicated
Outputs:
- output 1: bfloat16 [32, 1024, 2048], P(None, 'sp')
- output 2: bfloat16 [32, 1024, 2048], P(None, 'sp')
- output 3: float32 [2048, 2048], replicated
- output 4: float32 [2048, 128], replicated
- output 5: float32 [2048, 128], replicated
- output 6: float32 [2048, 2048], replicated
- output 7: float32 [2048], replicated
All inputs are finite; a program needn't handle non-finite values.
Results may differ from a plain program's by a relative error of at most 0.0115518.
Values are sent between devices in bfloat16 or wider.
A program may use at most 1 GiB of HBM per device.

v0:
```python
import jax
import jax.numpy as jnp
from jax import lax
from jax.sharding import PartitionSpec as P

ROPE_THETA = 10000.0
NORM_EPS = 1e-6
MASK_FILL = -1e30


def rope_tables(positions, head_dim):
    half = head_dim // 2
    frequencies = ROPE_THETA ** (-2.0 * jnp.arange(half, dtype=jnp.float32) / head_dim)
    angles = positions.astype(jnp.float32)[:, None] * frequencies[None, :]
    return jnp.cos(angles), jnp.sin(angles)


def apply_rope(vectors, cos_tab, sin_tab):
    half = vectors.shape[-1] // 2
    first = vectors[..., :half]
    second = vectors[..., half:]
    return jnp.concatenate([first * cos_tab - second * sin_tab, second * cos_tab + first * sin_tab], axis=-1)


def rms_norm(x_f32, gain):
    inv_rms = lax.rsqrt(jnp.mean(x_f32 * x_f32, axis=-1, keepdims=True) + NORM_EPS)
    return x_f32 * inv_rms * (1.0 + gain)


def visible_mask(prefix_len, query_pos, key_pos):
    key_grid = key_pos[None, None, None, :]
    return (key_grid < prefix_len[:, None, None, None]) | (key_grid <= query_pos[None, None, :, None])


def attend_forward(q_blk, k_all, v_all, visible):
    scores = jnp.einsum('bqhe,bke->bhqk', q_blk, k_all, preferred_element_type=jnp.float32)
    attn_probs = jax.nn.softmax(jnp.where(visible, scores, MASK_FILL), axis=-1).astype(jnp.bfloat16)
    return jnp.einsum('bhqk,bke->bqhe', attn_probs, v_all, preferred_element_type=jnp.float32).astype(jnp.bfloat16)


def attend_backward(q_blk, do_blk, k_all, v_all, visible):
    scores = jnp.einsum('bqhe,bke->bhqk', q_blk, k_all, preferred_element_type=jnp.float32)
    attn_probs = jax.nn.softmax(jnp.where(visible, scores, MASK_FILL), axis=-1)
    dprobs = jnp.einsum('bqhe,bke->bhqk', do_blk, v_all, preferred_element_type=jnp.float32).astype(jnp.bfloat16).astype(jnp.float32)
    row_delta = jnp.sum(dprobs * attn_probs, axis=-1, keepdims=True)
    dscores = (attn_probs * (dprobs - row_delta)).astype(jnp.bfloat16)
    dq_blk = jnp.einsum('bhqk,bke->bqhe', dscores, k_all, preferred_element_type=jnp.float32).astype(jnp.bfloat16)
    dk_part = jnp.einsum('bhqk,bqhe->bke', dscores, q_blk, preferred_element_type=jnp.float32)
    dv_part = jnp.einsum('bhqk,bqhe->bke', attn_probs.astype(jnp.bfloat16), do_blk, preferred_element_type=jnp.float32)
    return dq_blk, dk_part, dv_part


def solution(mesh):
    groups = mesh.shape['sp']
    seq_spec = P(None, 'sp', None)
    whole = P()

    def local_block(x, dy, prefix_len, w_norm, w_q, w_k, w_v, w_o):
        batch, seq_dev, d_model = x.shape
        head_dim = w_k.shape[1]
        heads = w_q.shape[1] // head_dim
        local_heads = heads // groups
        scale = head_dim ** -0.5
        my_index = lax.axis_index('sp')
        w_q4 = w_q.reshape(d_model, groups, local_heads, head_dim)
        w_o4 = w_o.reshape(groups, local_heads, head_dim, d_model)

        x_f32 = x.astype(jnp.float32)
        normed_f32, norm_pull = jax.vjp(rms_norm, x_f32, w_norm.astype(jnp.float32))
        normed = normed_f32.astype(jnp.bfloat16)
        own_pos = my_index * seq_dev + jnp.arange(seq_dev)
        cos_tab, sin_tab = rope_tables(own_pos, head_dim)
        cos_q = cos_tab[None, None, :, None, :]
        sin_q = sin_tab[None, None, :, None, :]
        q_proj = jnp.einsum('bsd,dghe->gbshe', normed, w_q4, preferred_element_type=jnp.float32)
        q_send = (apply_rope(q_proj, cos_q, sin_q) * scale).astype(jnp.bfloat16)
        k_own = apply_rope(jnp.einsum('bsd,de->bse', normed, w_k, preferred_element_type=jnp.float32), cos_tab, sin_tab).astype(jnp.bfloat16)
        v_own = jnp.einsum('bsd,de->bse', normed, w_v, preferred_element_type=jnp.float32).astype(jnp.bfloat16)

        q_heads = lax.all_to_all(q_send, 'sp', 0, 0, tiled=True)
        k_all = lax.all_gather(k_own, 'sp', axis=1, tiled=True)
        v_all = lax.all_gather(v_own, 'sp', axis=1, tiled=True)
        key_pos = jnp.arange(seq_dev * groups)
        block_ids = jnp.arange(groups)

        def forward_block(item):
            q_blk, block_id = item
            visible = visible_mask(prefix_len, block_id * seq_dev + jnp.arange(seq_dev), key_pos)
            return attend_forward(q_blk, k_all, v_all, visible)

        o_heads = lax.map(forward_block, (q_heads, block_ids))
        o_seq = lax.all_to_all(o_heads, 'sp', 0, 0, tiled=True)
        mixed = jnp.einsum('gbshe,ghed->bsd', o_seq, w_o4, preferred_element_type=jnp.float32)
        y_out = (x_f32 + mixed).astype(jnp.bfloat16)

        d_wo = jnp.einsum('gbshe,bsd->ghed', o_seq, dy, preferred_element_type=jnp.float32).reshape(heads * head_dim, d_model)
        do_send = jnp.einsum('bsd,ghed->gbshe', dy, w_o4, preferred_element_type=jnp.float32).astype(jnp.bfloat16)
        do_heads = lax.all_to_all(do_send, 'sp', 0, 0, tiled=True)

        def backward_block(carry, item):
            dk_acc, dv_acc = carry
            q_blk, do_blk, block_id = item
            visible = visible_mask(prefix_len, block_id * seq_dev + jnp.arange(seq_dev), key_pos)
            dq_blk, dk_part, dv_part = attend_backward(q_blk, do_blk, k_all, v_all, visible)
            return (dk_acc + dk_part, dv_acc + dv_part), dq_blk

        kv_zero = jnp.zeros((batch, seq_dev * groups, head_dim), jnp.float32)
        (dk_full, dv_full), dq_heads = lax.scan(backward_block, (kv_zero, kv_zero), (q_heads, do_heads, block_ids))
        dq_seq = lax.all_to_all(dq_heads, 'sp', 0, 0, tiled=True)
        dk_own = lax.psum_scatter(dk_full, 'sp', scatter_dimension=1, tiled=True).astype(jnp.bfloat16)
        dv_own = lax.psum_scatter(dv_full, 'sp', scatter_dimension=1, tiled=True).astype(jnp.bfloat16)

        dq_proj = apply_rope(dq_seq.astype(jnp.float32) * scale, cos_q, -sin_q).astype(jnp.bfloat16)
        dk_proj = apply_rope(dk_own.astype(jnp.float32), cos_tab, -sin_tab).astype(jnp.bfloat16)
        d_wq = jnp.einsum('bsd,gbshe->dghe', normed, dq_proj, preferred_element_type=jnp.float32).reshape(d_model, heads * head_dim)
        d_wk = jnp.einsum('bsd,bse->de', normed, dk_proj, preferred_element_type=jnp.float32)
        d_wv = jnp.einsum('bsd,bse->de', normed, dv_own, preferred_element_type=jnp.float32)
        d_normed = (jnp.einsum('gbshe,dghe->bsd', dq_proj, w_q4, preferred_element_type=jnp.float32) + jnp.einsum('bse,de->bsd', dk_proj, w_k, preferred_element_type=jnp.float32) + jnp.einsum('bse,de->bsd', dv_own, w_v, preferred_element_type=jnp.float32))
        dx_norm, d_gain = norm_pull(d_normed.astype(jnp.bfloat16).astype(jnp.float32))
        dx_out = (dy.astype(jnp.float32) + dx_norm).astype(jnp.bfloat16)
        d_wq, d_wk, d_wv, d_wo, d_gain = lax.psum((d_wq, d_wk, d_wv, d_wo, d_gain), 'sp')
        return y_out, dx_out, d_wq, d_wk, d_wv, d_wo, d_gain

    return jax.shard_map(local_block, mesh=mesh, in_specs=(seq_spec, seq_spec, whole, whole, whole, whole, whole, whole), out_specs=(seq_spec, seq_spec, whole, whole, whole, whole, whole), check_vma=False)
```

profile of v0, /device:TPU:0, one launch (start us, length us, event | category | flops | bytes accessed | tf_op | source)
XLA Modules:
  0.0 3412.8 jit_solution(17974558668651317003)
XLA Ops:
  61.7 42.7 %fusion.73 = f32[8,32,128,2,128]{2,4,3,0,1:T(8,128)} fusion(bf16[2048,8,2,128]{0,3,2,1:T(8,128)(2,1)} %copy.38, bf16[32,128,2048]{2,1,0:T(8,128)(2,1)} %param.12, f32[2048]{0:T(1024)S(1)} %convert_add_fusion.1, f32[32,128]{1,0:T(8,128)S(1)} %fusion.90), kind=kOutput, calls=%fused_computation.101 | convolution fusion | flops 34393292800 | bytes 58744832 | tf_op jit(solution)/shard_map/bsd,dghe->gbshe/dot_general | solution.py:75
  165.3 41.2 %convert_bitcast_fusion.1 = bf16[8,32,128,2,128]{2,4,1,3,0:T(8,128)(2,1)} fusion(bf16[8,2,128,2048,1]{3,2,4,1,0:T(8,128)(2,1)} %bitcast.235, bf16[32,128,2048]{2,1,0:T(8,128)(2,1)} %param.13), kind=kOutput, calls=%fused_computation.98 | convolution fusion | flops 34368126976 | bytes 41943040 | tf_op jit(solution)/shard_map/bsd,ghed->gbshe/dot_general | solution.py:97
  206.5 167.8 %all-to-all-done = bf16[8,32,128,2,128]{2,4,3,1,0:T(8,128)(2,1)} async-done(((bf16[8,32,128,2,128]{2,4,3,1,0:T(8,128)(2,1)}), bf16[8,32,128,2,128]{2,4,3,1,0:T(8,128)(2,1)}, u32[]{:S(2)}, u32[]{:S(2)}) %all-to-all-start) | async-done | bytes 16777248 | tf_op jit(solution)/shard_map/all_to_all | solution.py:80
  412.1 150.7 %all-to-all-done.2 = bf16[8,32,128,2,128]{2,4,1,3,0:T(8,128)(2,1)} async-done(((bf16[8,32,128,2,128]{2,4,1,3,0:T(8,128)(2,1)}), bf16[8,32,128,2,128]{2,4,1,3,0:T(8,128)(2,1)}, u32[]{:S(2)}, u32[]{:S(2)}) %all-to-all-start.2) | async-done | bytes 16777248 | tf_op jit(solution)/shard_map/all_to_all | solution.py:98
  562.7 1382.4 %while.29 = (s32[]{:T(128)}, f32[32,1024,128]{2,1,0:T(8,128)}, f32[32,1024,128]{2,1,0:T(8,128)}, bf16[8,32,128,2,128]{2,4,3,1,0:T(8,128)(2,1)}, s32[32]{0:T(128)...) while((s32[]{:T(128)}, f32[32,1024,128]{2,1,0:T(8,128)}, ...), condition=%wide.region_9.10_spmd.clone.clone, body=%wide.region_5.9_spmd.clone.clone.sunk | while | flops 10893812736 | bytes 422055008 | solution.py:108
  766.4 39.5 %fusion.147 = (f32[32,2,128]{2,1,0:T(2,128)S(1)}, f32[32,2,128,1024]{3,2,1,0:T(8,128)}) fusion(f32[32,128,2,1024]{3,1,2,0:T(8,128)} %fusion.146, pred[32,128,1024]{2,1,0:T(8,128)(4,1)} %broadcast_or_fusion.5), kind=kOutput, calls=%fused_computation.138.clone.1 | output fusion | flops 33555456 | bytes 71335936 | tf_op jit(solution)/shard_map/while/body/eval_jaxpr/sub | solution.py:43
  938.1 39.5 %fusion.147 = (f32[32,2,128]{2,1,0:T(2,128)S(1)}, f32[32,2,128,1024]{3,2,1,0:T(8,128)}) fusion(f32[32,128,2,1024]{3,1,2,0:T(8,128)} %fusion.146, pred[32,128,1024]{2,1,0:T(8,128)(4,1)} %broadcast_or_fusion.5), kind=kOutput, calls=%fused_computation.138.clone.1 | output fusion | flops 33555456 | bytes 71335936 | tf_op jit(solution)/shard_map/while/body/eval_jaxpr/sub | solution.py:43
  1109.8 39.5 %fusion.147 = (f32[32,2,128]{2,1,0:T(2,128)S(1)}, f32[32,2,128,1024]{3,2,1,0:T(8,128)}) fusion(f32[32,128,2,1024]{3,1,2,0:T(8,128)} %fusion.146, pred[32,128,1024]{2,1,0:T(8,128)(4,1)} %broadcast_or_fusion.5), kind=kOutput, calls=%fused_computation.138.clone.1 | output fusion | flops 33555456 | bytes 71335936 | tf_op jit(solution)/shard_map/while/body/eval_jaxpr/sub | solution.py:43
  1796.4 39.5 %fusion.147 = (f32[32,2,128]{2,1,0:T(2,128)S(1)}, f32[32,2,128,1024]{3,2,1,0:T(8,128)}) fusion(f32[32,128,2,1024]{3,1,2,0:T(8,128)} %fusion.146, pred[32,128,1024]{2,1,0:T(8,128)(4,1)} %broadcast_or_fusion.5), kind=kOutput, calls=%fused_computation.138.clone.1 | output fusion | flops 33555456 | bytes 71335936 | tf_op jit(solution)/shard_map/while/body/eval_jaxpr/sub | solution.py:43
  1967.1 638.6 %while.28 = (s32[]{:T(128)}, bf16[8,32,128,2,128]{4,2,3,1,0:T(8,128)(2,1)}, s32[32]{0:T(128)}, s32[8]{0:T(128)S(1)}, bf16[8,32,128,2,128]{4,2,3,1,0:T(8,128)(2,1...) while((s32[]{:T(128)}, ...), condition=%wide.region_4.5_spmd.clone.clone, body=%wide.region_1.4_spmd.clone.clone.sunk | while | flops 4350706688 | bytes 163973360 | solution.py:91
  1990.6 39.6 %fusion.137 = (f32[32,2,128]{2,1,0:T(2,128)S(1)}, f32[32,2,128,1024]{3,2,1,0:T(8,128)}) fusion(f32[32,128,2,1024]{3,1,2,0:T(8,128)} %fusion.136, pred[32,128,1024]{2,1,0:T(8,128)(4,1)} %broadcast_or_fusion.4), kind=kOutput, calls=%fused_computation.137.clone.1 | output fusion | flops 33555456 | bytes 71335936 | tf_op jit(solution)/shard_map/while/body/eval_jaxpr/sub | solution.py:37
  2070.4 39.6 %fusion.137 = (f32[32,2,128]{2,1,0:T(2,128)S(1)}, f32[32,2,128,1024]{3,2,1,0:T(8,128)}) fusion(f32[32,128,2,1024]{3,1,2,0:T(8,128)} %fusion.136, pred[32,128,1024]{2,1,0:T(8,128)(4,1)} %broadcast_or_fusion.4), kind=kOutput, calls=%fused_computation.137.clone.1 | output fusion | flops 33555456 | bytes 71335936 | tf_op jit(solution)/shard_map/while/body/eval_jaxpr/sub | solution.py:37
  2150.2 39.6 %fusion.137 = (f32[32,2,128]{2,1,0:T(2,128)S(1)}, f32[32,2,128,1024]{3,2,1,0:T(8,128)}) fusion(f32[32,128,2,1024]{3,1,2,0:T(8,128)} %fusion.136, pred[32,128,1024]{2,1,0:T(8,128)(4,1)} %broadcast_or_fusion.4), kind=kOutput, calls=%fused_computation.137.clone.1 | output fusion | flops 33555456 | bytes 71335936 | tf_op jit(solution)/shard_map/while/body/eval_jaxpr/sub | solution.py:37
  2230.0 39.6 %fusion.137 = (f32[32,2,128]{2,1,0:T(2,128)S(1)}, f32[32,2,128,1024]{3,2,1,0:T(8,128)}) fusion(f32[32,128,2,1024]{3,1,2,0:T(8,128)} %fusion.136, pred[32,128,1024]{2,1,0:T(8,128)(4,1)} %broadcast_or_fusion.4), kind=kOutput, calls=%fused_computation.137.clone.1 | output fusion | flops 33555456 | bytes 71335936 | tf_op jit(solution)/shard_map/while/body/eval_jaxpr/sub | solution.py:37
  2309.8 39.6 %fusion.137 = (f32[32,2,128]{2,1,0:T(2,128)S(1)}, f32[32,2,128,1024]{3,2,1,0:T(8,128)}) fusion(f32[32,128,2,1024]{3,1,2,0:T(8,128)} %fusion.136, pred[32,128,1024]{2,1,0:T(8,128)(4,1)} %broadcast_or_fusion.4), kind=kOutput, calls=%fused_computation.137.clone.1 | output fusion | flops 33555456 | bytes 71335936 | tf_op jit(solution)/shard_map/while/body/eval_jaxpr/sub | solution.py:37
  2389.7 39.6 %fusion.137 = (f32[32,2,128]{2,1,0:T(2,128)S(1)}, f32[32,2,128,1024]{3,2,1,0:T(8,128)}) fusion(f32[32,128,2,1024]{3,1,2,0:T(8,128)} %fusion.136, pred[32,128,1024]{2,1,0:T(8,128)(4,1)} %broadcast_or_fusion.4), kind=kOutput, calls=%fused_computation.137.clone.1 | output fusion | flops 33555456 | bytes 71335936 | tf_op jit(solution)/shard_map/while/body/eval_jaxpr/sub | solution.py:37
  2469.5 39.6 %fusion.137 = (f32[32,2,128]{2,1,0:T(2,128)S(1)}, f32[32,2,128,1024]{3,2,1,0:T(8,128)}) fusion(f32[32,128,2,1024]{3,1,2,0:T(8,128)} %fusion.136, pred[32,128,1024]{2,1,0:T(8,128)(4,1)} %broadcast_or_fusion.4), kind=kOutput, calls=%fused_computation.137.clone.1 | output fusion | flops 33555456 | bytes 71335936 | tf_op jit(solution)/shard_map/while/body/eval_jaxpr/sub | solution.py:37
  2549.3 39.6 %fusion.137 = (f32[32,2,128]{2,1,0:T(2,128)S(1)}, f32[32,2,128,1024]{3,2,1,0:T(8,128)}) fusion(f32[32,128,2,1024]{3,1,2,0:T(8,128)} %fusion.136, pred[32,128,1024]{2,1,0:T(8,128)(4,1)} %broadcast_or_fusion.4), kind=kOutput, calls=%fused_computation.137.clone.1 | output fusion | flops 33555456 | bytes 71335936 | tf_op jit(solution)/shard_map/while/body/eval_jaxpr/sub | solution.py:37
  2646.6 46.1 %fusion.67 = f32[2048,8,2,128,1]{0,3,2,1,4:T(8,128)} fusion(bf16[8,32,128,2,64]{2,4,3,0,1:T(8,128)(2,1)} %get-tuple-element.296, bf16[8,32,128,2,64]{2,4,3,0,1:T(8,128)(2,1)} %get-tuple-element.295, bf16[32,128,2048]{2,1,0:T(8,128)(2,1)} %param.12, f32[2048]{0:T(1024)S(1)} %copy-done.18, f32[32,128]{1,0:T(8,128)S(1)} %copy-done.15), kind=kOutput, calls=%fused_computation.90 | convolution fusion | flops 34426847232 | bytes 50356224 | tf_op jit(solution)/shard_map/bsd,gbshe->dghe/dot_general | solution.py:115
  2710.3 151.1 %all-to-all-done.1 = bf16[8,32,128,2,128]{4,2,3,1,0:T(8,128)(2,1)} async-done(((bf16[8,32,128,2,128]{4,2,3,1,0:T(8,128)(2,1)}), bf16[8,32,128,2,128]{4,2,3,1,0:T(8,128)(2,1)}, u32[]{:S(2)}, u32[]{:S(2)}) %all-to-all-start.1) | async-done | bytes 16777248 | tf_op jit(solution)/shard_map/all_to_all | solution.py:92
  2861.4 43.7 %fusion.65 = f32[8,2,128,2048,1]{3,2,1,4,0:T(8,128)} fusion(bf16[8,32,128,2,128]{4,2,3,1,0:T(8,128)(2,1)} %all-to-all-done.1, bf16[32,128,2048]{2,1,0:T(8,128)(2,1)} %param.13), kind=kOutput, calls=%fused_computation.87 | convolution fusion | flops 34359738368 | bytes 50331648 | tf_op jit(solution)/shard_map/gbshe,bsd->ghed/dot_general | solution.py:96
  2905.2 41.9 %fusion.60 = bf16[32,128,2048]{2,1,0:T(8,128)(2,1)} fusion(bf16[32,128,2048]{2,1,0:T(8,128)(2,1)} %param.12, bf16[8,32,128,2,128]{4,2,3,1,0:T(8,128)(2,1)} %all-to-all-done.1, bf16[8,2,128,2048,1]{3,2,1,4,0:T(8,128)(2,1)} %bitcast.236), kind=kOutput, calls=%fused_computation.79 | convolution fusion | flops 34384904192 | bytes 58720256 | tf_op jit(solution)/shard_map/gbshe,ghed->bsd/dot_general | solution.py:93
  2973.0 44.0 %fusion.76 = f32[32,128,2048,1,1]{2,1,4,3,0:T(8,128)} fusion(bf16[8,32,128,2,64]{2,4,3,0,1:T(8,128)(2,1)} %get-tuple-element.296, bf16[8,32,128,2,64]{2,4,3,0,1:T(8,128)(2,1)} %get-tuple-element.295, bf16[2048,8,2,128,1]{3,2,1,0,4:T(2,128)(2,1)} %bitcast.232), kind=kOutput, calls=%fused_computation.102 | convolution fusion | flops 34393292800 | bytes 58720256 | tf_op jit(solution)/shard_map/gbshe,dghe->bsd/dot_general | solution.py:118
  3113.3 268.8 %all-reduce.3.cloned.1.call-done = (f32[2048,2048]{1,0:T(8,128)}, f32[2048,128]{1,0:T(8,128)}, f32[2048,128]{1,0:T(8,128)}, f32[2048,2048]{1,0:T(8,128)}) async-done(((f32[2048,2048]{1,0:T(8,128)}, f32[2048,128]{1,0:T(8,128)}, f32[2048,128]{1,0:T(8,128)}, f32[2048,2048]{1,0:T(8,128)}), (f32[2048,2048]{1,0:T(8,128)}, f32[2048,128]{1,0:T(8,128)}, f32[2048,128]{1,0:T(8,128)}, ...) | async-done | bytes 35651600 | tf_op jit(solution)/shard_map/psum | solution.py:121
  (327 shorter events, 1900.3 us)
Async XLA Ops:
  7.2 148.9 %copy-start = (bf16[2048,128]{1,0:T(8,128)(2,1)S(1)}, bf16[2048,128]{1,0:T(8,128)(2,1)}, u32[]{:S(2)}) copy-start(bf16[2048,128]{1,0:T(8,128)(2,1)} %param.18) | copy-start | bytes 1572868
  7.2 392.9 %all-gather.3.cloned.1.call-start = ((), (), s32[]{:S(2)}) async-start(), calls=%async_computation.6 | async-start | bytes 9437184 | tf_op jit(solution)/shard_map/all_gather | solution.py:81
  15.2 140.9 %copy-start.14 = (f32[32,128]{1,0:T(8,128)}, f32[32,128]{1,0:T(8,128)S(1)}, u32[]{:S(2)}) copy-start(f32[32,128]{1,0:T(8,128)S(1)} %fusion.90) | copy-start | bytes 49156
  15.2 140.9 %copy-start.17 = (f32[2048]{0:T(1024)}, f32[2048]{0:T(1024)S(1)}, u32[]{:S(2)}) copy-start(f32[2048]{0:T(1024)S(1)} %convert_add_fusion.1) | copy-start | bytes 24580
  16.0 88.4 %copy-start.5 = (f32[128,64]{0,1:T(8,128)}, f32[128,64]{0,1:T(8,128)S(1)}, u32[]{:S(2)}) copy-start(f32[128,64]{0,1:T(8,128)S(1)} %get-tuple-element.305) | copy-start | bytes 98308
  151.2 223.1 %all-to-all-start = ((bf16[8,32,128,2,128]{2,4,3,1,0:T(8,128)(2,1)}), bf16[8,32,128,2,128]{2,4,3,1,0:T(8,128)(2,1)}, u32[]{:S(2)}, u32[]{:S(2)}) async-start(bf16[8,32,128,2,128]{2,4,3,1,0:T(8,128)(2,1)} %copy.39), calls=%async_computation | async-start | bytes 33554432 | tf_op jit(solution)/shard_map/all_to_all | solution.py:80
  155.6 256.4 %all-gather.5.cloned.1.call-start = ((), (), s32[]{:S(2)}) async-start(), calls=%async_computation.7 | async-start | bytes 9437184 | tf_op jit(solution)/shard_map/all_gather | solution.py:82
  374.3 188.4 %all-to-all-start.2 = ((bf16[8,32,128,2,128]{2,4,1,3,0:T(8,128)(2,1)}), bf16[8,32,128,2,128]{2,4,1,3,0:T(8,128)(2,1)}, u32[]{:S(2)}, u32[]{:S(2)}) async-start(bf16[8,32,128,2,128]{2,4,1,3,0:T(8,128)(2,1)} %convert_bitcast_fusion.1), calls=%async_computation.2 | async-start | bytes 33554432 | tf_op jit(solution)/shard_map/all_to_all | solution.py:98
  378.8 2568.3 %reduce-scatter.3.cloned.1.call-start = ((), (), s32[]{:S(2)}) async-start(), calls=%async_computation.8 | async-start | bytes 18874368 | tf_op jit(solution)/shard_map/reduce_scatter | solution.py:110
  1153.8 25.6 copy-start.1
  1325.4 25.6 copy-start.1
  1497.1 25.6 copy-start.1
  1668.8 25.6 copy-start.1
  1840.4 25.6 copy-start.1
  1962.6 643.1 %all-to-all-start.3 = ((bf16[8,32,128,2,128]{2,4,3,1,0:T(8,128)(2,1)}), bf16[8,32,128,2,128]{2,4,3,1,0:T(8,128)(2,1)}, u32[]{:S(2)}, u32[]{:S(2)}) async-start(bf16[8,32,128,2,128]{2,4,3,1,0:T(8,128)(2,1)} %get-tuple-element.115), calls=%async_computation.3 | async-start | bytes 33554432 | tf_op jit(solution)/shard_map/all_to_all | solution.py:109
  1967.1 992.7 %reduce-scatter.5.cloned.1.call-start = ((), (), s32[]{:S(2)}) async-start(), calls=%async_computation.9 | async-start | bytes 18874368 | tf_op jit(solution)/shard_map/reduce_scatter | solution.py:111
  2605.7 255.7 %all-to-all-start.1 = ((bf16[8,32,128,2,128]{4,2,3,1,0:T(8,128)(2,1)}), bf16[8,32,128,2,128]{4,2,3,1,0:T(8,128)(2,1)}, u32[]{:S(2)}, u32[]{:S(2)}) async-start(bf16[8,32,128,2,128]{4,2,3,1,0:T(8,128)(2,1)} %get-tuple-element.114), calls=%async_computation.1 | async-start | bytes 33554432 | tf_op jit(solution)/shard_map/all_to_all | solution.py:92
  2610.2 771.9 %all-reduce.3.cloned.1.call-start = ((), (), s32[]{:S(2)}) async-start(), calls=%async_computation.10 | async-start | bytes 71303168 | tf_op jit(solution)/shard_map/psum | solution.py:121
  2905.2 43.7 %copy-start.7 = (f32[128,64]{0,1:T(8,128)S(1)}, f32[128,64]{0,1:T(8,128)}, u32[]{:S(2)}) copy-start(f32[128,64]{0,1:T(8,128)} %copy-done.5) | copy-start | bytes 98308
  2905.2 43.7 %copy-start.11 = (f32[128,64]{0,1:T(8,128)S(1)}, f32[128,64]{0,1:T(8,128)}, u32[]{:S(2)}) copy-start(f32[128,64]{0,1:T(8,128)} %get-tuple-element.303) | copy-start | bytes 98308
  2905.2 44.0 %copy-start.16 = (f32[32,128]{1,0:T(8,128)S(1)}, f32[32,128]{1,0:T(8,128)}, u32[]{:S(2)}) copy-start(f32[32,128]{1,0:T(8,128)} %copy-done.14) | copy-start | bytes 49156
  2905.2 44.0 %copy-start.19 = (f32[2048]{0:T(1024)S(1)}, f32[2048]{0:T(1024)}, u32[]{:S(2)}) copy-start(f32[2048]{0:T(1024)} %copy-done.17) | copy-start | bytes 24580
  2973.0 44.0 %copy-start.9 = (bf16[2048,128]{1,0:T(8,128)(2,1)S(1)}, bf16[2048,128]{1,0:T(8,128)(2,1)}, u32[]{:S(2)}) copy-start(bf16[2048,128]{1,0:T(8,128)(2,1)} %param.17) | copy-start | bytes 1572868
  3030.1 58.3 %copy-start.13 = (f32[32,128]{1,0:T(8,128)S(1)}, f32[32,128]{1,0:T(8,128)}, u32[]{:S(2)}) copy-start(f32[32,128]{1,0:T(8,128)} %copy-done.12) | copy-start | bytes 49156
  (29 other events, 488.4 us)
Sparse Core Ops, SparseCore 0:
  26.5 52.7 all-gather.2
  165.4 142.9 all-gather.4
  1962.7 240.0 reduce-scatter.2
  2605.9 240.1 reduce-scatter.4
  2973.1 408.9 all-reduce.2
where the time goes:
time: 3420 us; the launch traced here: 3410 us
  matrix products  1370 us (40%)
  other arithmetic  1000 us (29%)
  waiting for transfers between devices  739 us (22%)
  local copies, waits for them, and re-layouts  225 us (7%)
    sub x8, other arithmetic, attend_forward(): jax.nn.softmax(jnp.where(visible, scores, MASK_FILL), axis=-1)  317 us
    sub x8, other arithmetic, attend_backward(): attn_probs = jax.nn.softmax(jnp.where(visible, scores, MASK_FILL), axis=-1)  316 us
    psum x1, waiting for transfers between devices, local_block(): lax.psum((d_wq, d_wk, d_wv, d_wo, d_gain), 'sp')  269 us
    dot_general x8, matrix products, attend_backward(): jnp.einsum('bhqk,bqhe->bke', attn_probs.astype(jnp.bfloat16), do_blk, pre...  203 us
    convert_element_type x8, other arithmetic, attend_backward(): dscores = (attn_probs * (dprobs - row_delta)).astype(jnp.bfloat16)  180 us
    all_to_all x1, waiting for transfers between devices, local_block(): q_heads = lax.all_to_all(q_send, 'sp', 0, 0, tiled=True)  168 us
    dot_general x8, matrix products, attend_backward(): jnp.einsum('bqhe,bke->bhqk', do_blk, v_all, preferred_element_type=jnp.fl...  156 us
    all_to_all x1, waiting for transfers between devices, local_block(): o_seq = lax.all_to_all(o_heads, 'sp', 0, 0, tiled=True)  151 us
  transfers between devices with their start and end apart: 9, of which 4 were waited for; matrix products, arithmetic and copies ran while one was open for 34% of the time, Pallas kernels for 0%

commit v1 on v0

v1 whole, which is shorter than its diff:
```python
import functools

import jax
import jax.numpy as jnp
from jax import lax
from jax.experimental import pallas as pl
from jax.experimental.pallas import tpu as pltpu
from jax.sharding import PartitionSpec as P


ROPE_THETA = 10000.0
NORM_EPS = 1e-6
MASK_FILL = -1e30
F32 = jnp.float32
BF16 = jnp.bfloat16
MESH = pl.DeviceIdType.MESH
VMEM_LIMIT = 60 * 1024 * 1024
NT = (((1,), (1,)), ((), ()))


def mm(a, b):
    return jnp.dot(a, b, preferred_element_type=F32)


def mm_nt(a, b):
    return lax.dot_general(a, b, NT, preferred_element_type=F32)


def rotate(v, cos, sin):
    return v * cos + pltpu.roll(v, v.shape[-1] // 2, 1) * sin


def pre_kernel(x_ref, gain_ref, wq_ref, wkv_ref, cos_ref, sin_ref, xn_ref, q_ref, kv_ref, *, scale):
    nb, seq, d_model = x_ref.shape
    hd = cos_ref.shape[1]
    rows = nb * seq
    x = x_ref[...].reshape(rows, d_model).astype(F32)
    inv = lax.rsqrt(jnp.mean(x * x, axis=-1, keepdims=True) + NORM_EPS)
    xn_ref[...] = (x * inv * (1.0 + gain_ref[...])).astype(BF16).reshape(nb, seq, d_model)
    xn = xn_ref[...].reshape(rows, d_model)
    cos = jnp.concatenate([cos_ref[...]] * nb, axis=0)
    sin = jnp.concatenate([sin_ref[...]] * nb, axis=0)
    kv = mm(xn, wkv_ref[...])
    kv_ref[:, :, :hd] = rotate(kv[:, :hd], cos, sin).astype(BF16).reshape(nb, seq, hd)
    kv_ref[:, :, hd:] = kv[:, hd:].astype(BF16).reshape(nb, seq, hd)
    width = wq_ref.shape[1]
    step = 512
    for n in range(width // step):
        proj = mm(xn, wq_ref[:, n * step:(n + 1) * step])
        for h in range(step // hd):
            rot = rotate(proj[:, h * hd:(h + 1) * hd], cos, sin) * scale
            lo = n * step + h * hd
            q_ref[:, :, lo:lo + hd] = rot.astype(BF16).reshape(nb, seq, hd)


def attention_kernel(batch, prefix_ref, q_ref, do_ref, kv_ref, cos_ref, sin_ref, o_ref, dq_ref, dkv_ref,
                     s_scr, e_scr, dp_scr, k_ext, v_scr, k_t, v_t, eye_scr, top_scr, stat_scr,
                     part, recv1, sum1, recv2, sum2, recv3,
                     send1, got1, send2, got2, send3, got3, free1, free2, free3, *, scale):
    t = pl.program_id(0)
    me = lax.axis_index('sp')
    core = me % 2
    x_bit = (me // 2) % 2
    y_bit = me // 4
    partner = me + 1 - 2 * core
    x_near = me + 2 - 4 * x_bit
    y_near = me + 4 - 8 * y_bit
    near_1 = x_near * (1 - core) + y_near * core
    near_2 = y_near * (1 - core) + x_near * core
    bit_1 = x_bit * (1 - core) + y_bit * core
    bit_2 = y_bit * (1 - core) + x_bit * core

    groups, _, seq, _ = kv_ref.shape
    hd = kv_ref.shape[3] // 2
    keys = groups * seq
    pairs = q_ref.shape[2] // (2 * hd)
    chunk = 256

    def copy_1(slot):
        return pltpu.make_async_remote_copy(part.at[slot, 1 - core], recv1.at[slot], send1.at[slot], got1.at[slot],
                                            device_id=(partner,), device_id_type=MESH)

    def copy_2(slot):
        return pltpu.make_async_remote_copy(sum1.at[slot, 1 - bit_1], recv2.at[slot], send2.at[slot], got2.at[slot],
                                            device_id=(near_1,), device_id_type=MESH)

    def copy_3(slot):
        return pltpu.make_async_remote_copy(sum2.at[slot, 1 - bit_2], recv3.at[slot], send3.at[slot], got3.at[slot],
                                            device_id=(near_2,), device_id_type=MESH)

    @pl.when(t == 0)
    def _():
        barrier = pltpu.get_barrier_semaphore()
        for other in (partner, near_1, near_2):
            pl.semaphore_signal(barrier, inc=1, device_id=(other,), device_id_type=MESH)
        pl.semaphore_wait(barrier, 3)

    @pl.when(t == 0)
    def _():
        eye_scr[...] = (lax.broadcasted_iota(jnp.int32, (seq, seq), 0)
                        == lax.broadcasted_iota(jnp.int32, (seq, seq), 1)).astype(F32).astype(BF16)

    def fold(a, op):
        return op(a.reshape(chunk // 8, 8, 2 * hd), axis=0)

    def heads_of(ref, lo):
        return jnp.concatenate([ref[0, :, pl.ds(lo, hd)], ref[0, :, pl.ds(lo + hd, hd)]], axis=0)

    def masked_q(lo):
        eye = eye_scr[...]
        return jnp.concatenate([heads_of(q_ref, lo), jnp.concatenate([eye, eye], axis=0)], axis=1)

    low = functools.partial(jnp.full, (8, 2 * hd), MASK_FILL, F32)

    @pl.when(t < batch)
    def _():
        slot = t % 2
        k_all = kv_ref[:, 0, :, :hd].reshape(keys, hd)
        v_all = kv_ref[:, 0, :, hd:].reshape(keys, hd)
        limit = jnp.maximum(prefix_ref[0, 0:1, :], me * seq + lax.broadcasted_iota(jnp.int32, (keys, seq), 1) + 1)
        k_ext[:, :hd] = k_all
        k_ext[:, hd:] = jnp.where(lax.broadcasted_iota(jnp.int32, (keys, seq), 0) < limit, 0.0, MASK_FILL).astype(BF16)
        v_scr[...] = v_all
        k_t[...] = k_all.T
        v_t[...] = v_all.T
        part[slot] = jnp.zeros(part.shape[1:], F32)

        def at_pair(i):
            return pl.multiple_of(i * 2 * hd, 2 * hd) if not isinstance(i, int) else i * 2 * hd

        def score_step(i, buf):
            q_ext = masked_q(at_pair(i))
            top = low()
            for c in range(keys // chunk):
                at = slice(c * chunk, (c + 1) * chunk)
                s = mm_nt(k_ext[at, :], q_ext)
                s_scr[buf, at, :] = s
                top = jnp.maximum(top, fold(s, jnp.max))
            top_scr[buf] = top

        def weigh_step(i, buf):
            do2 = heads_of(do_ref, at_pair(i))
            top = jnp.max(top_scr[buf], axis=0, keepdims=True)
            total = jnp.zeros((8, 2 * hd), F32)
            cross = jnp.zeros((8, 2 * hd), F32)
            for c in range(keys // chunk):
                at = slice(c * chunk, (c + 1) * chunk)
                dp = mm_nt(v_scr[at, :], do2).astype(BF16).astype(F32)
                e = jnp.exp(s_scr[buf, at, :] - top)
                e_scr[buf, at, :] = e
                dp_scr[buf, at, :] = dp
                total = total + fold(e, jnp.sum)
                cross = cross + fold(e * dp, jnp.sum)
            inv = 1.0 / jnp.sum(total, axis=0, keepdims=True)
            stat_scr[buf, 0:1, :] = inv
            stat_scr[buf, 1:2, :] = jnp.sum(cross, axis=0, keepdims=True) * inv

        def grad_step(i, buf):
            lo = at_pair(i)
            q2 = heads_of(q_ref, lo)
            do2 = heads_of(do_ref, lo)
            inv = stat_scr[buf, 0:1, :]
            delta = stat_scr[buf, 1:2, :]
            ps, dss = [], []
            for c in range(keys // chunk):
                at = slice(c * chunk, (c + 1) * chunk)
                p = e_scr[buf, at, :] * inv
                ds = (p * (dp_scr[buf, at, :] - delta)).astype(BF16)
                p = p.astype(BF16)
                ps.append(p)
                dss.append(ds)
                dk = mm(ds, q2)
                dv = mm(p, do2)
                for r in range(chunk // seq):
                    j = c * (chunk // seq) + r
                    part[slot, j % 2, j // 2, 0] += dk[r * seq:(r + 1) * seq, :]
                    part[slot, j % 2, j // 2, 1] += dv[r * seq:(r + 1) * seq, :]
            o_t = mm(v_t[...], jnp.concatenate(ps, axis=0)).astype(BF16)
            dq_t = mm(k_t[...], jnp.concatenate(dss, axis=0)).astype(BF16)
            for half in range(2):
                o_ref[0, :, pl.ds(lo + half * hd, hd)] = o_t[:, half * hd:(half + 1) * hd].T
                dq = dq_t[:, half * hd:(half + 1) * hd].T.astype(F32) * scale
                dq_ref[0, :, pl.ds(lo + half * hd, hd)] = rotate(dq, cos_ref[...], -sin_ref[...]).astype(BF16)

        def two_pairs(r, carry):
            i = 2 * r + 1
            score_step(i + 1, 0)
            weigh_step(i, 1)
            grad_step(i - 1, 0)
            score_step(i + 2, 1)
            weigh_step(i + 1, 0)
            grad_step(i, 1)
            return carry

        score_step(0, 0)
        score_step(1, 1)
        weigh_step(0, 0)
        lax.fori_loop(0, pairs // 2 - 1, two_pairs, 0)
        weigh_step(pairs - 1, 1)
        grad_step(pairs - 2, 0)
        grad_step(pairs - 1, 1)

    @pl.when(t >= 3)
    def _():
        slot = (t - 3) % 2
        copy_3(slot).wait()
        done = sum2[slot, bit_2] + recv3[slot]
        dkv_ref[0, :, :hd] = done[0]
        dkv_ref[0, :, hd:] = done[1]

        @pl.when(t - 3 < batch - 2)
        def _():
            pl.semaphore_signal(free3.at[slot], inc=1, device_id=(near_2,), device_id_type=MESH)

    @pl.when((t >= 2) & (t - 2 < batch))
    def _():
        slot = t % 2
        copy_2(slot).wait()
        for s in range(2):
            sum2[slot, s] = sum1[slot, bit_1, s] + recv2[slot, s]

        @pl.when(t - 2 < batch - 2)
        def _():
            pl.semaphore_signal(free2.at[slot], inc=1, device_id=(near_1,), device_id_type=MESH)

        @pl.when(t - 2 >= 2)
        def _():
            pl.semaphore_wait(free3.at[slot], 1)

        copy_3(slot).start()

    @pl.when((t >= 1) & (t - 1 < batch))
    def _():
        slot = (t - 1) % 2
        copy_1(slot).wait()
        for f in range(2):
            for s in range(2):
                chip = f * (1 + core) + s * (2 - core)
                sum1[slot, f, s] = part[slot, core, chip] + recv1[slot, chip]

        @pl.when(t - 1 < batch - 2)
        def _():
            pl.semaphore_signal(free1.at[slot], inc=1, device_id=(partner,), device_id_type=MESH)

        @pl.when(t - 1 >= 2)
        def _():
            pl.semaphore_wait(free2.at[slot], 1)

        copy_2(slot).start()

    @pl.when(t < batch)
    def _():
        slot = t % 2

        @pl.when(t >= 2)
        def _():
            pl.semaphore_wait(free1.at[slot], 1)

        copy_1(slot).start()


def post_kernel(dq_ref, dkv_ref, wq_ref, wkv_ref, x_ref, dy_ref, gain_ref, dx_ref, dgain_ref):
    nb, seq, d_model = x_ref.shape
    rows = nb * seq
    acc = mm_nt(dq_ref[...].reshape(rows, dq_ref.shape[2]), wq_ref[...])
    acc = acc + mm_nt(dkv_ref[...].reshape(rows, dkv_ref.shape[2]), wkv_ref[...])
    g = acc.astype(BF16).astype(F32)
    x = x_ref[...].reshape(rows, d_model).astype(F32)
    inv = lax.rsqrt(jnp.mean(x * x, axis=-1, keepdims=True) + NORM_EPS)
    xr = x * inv
    part = jnp.sum((g * xr).reshape(rows // 8, 8, d_model), axis=0)
    u = g * (1.0 + gain_ref[...])
    mean = jnp.mean(u * xr, axis=-1, keepdims=True)
    dy = dy_ref[...].reshape(rows, d_model).astype(F32)
    dx_ref[...] = (dy + inv * (u - xr * mean)).astype(BF16).reshape(nb, seq, d_model)

    @pl.when(pl.program_id(0) == 0)
    def _():
        dgain_ref[...] = jnp.zeros_like(dgain_ref)

    dgain_ref[...] += part


def solution(mesh):
    groups = mesh.shape['sp']
    seq_spec = P(None, 'sp', None)
    whole = P()

    def local_block(x, dy, prefix_len, w_norm, w_q, w_k, w_v, w_o):
        batch, seq, d_model = x.shape
        hd = w_k.shape[1]
        width = w_q.shape[1]
        keys = seq * groups
        tokens = batch * seq
        scale = hd ** -0.5
        me = lax.axis_index('sp')
        half = hd // 2
        freq = ROPE_THETA ** (-2.0 * jnp.arange(half, dtype=F32) / hd)
        angles = (me * seq + jnp.arange(seq)).astype(F32)[:, None] * freq[None, :]
        cos, sin = jnp.cos(angles), jnp.sin(angles)
        cos2 = jnp.concatenate([cos, cos], axis=1)
        sin2 = jnp.concatenate([-sin, sin], axis=1)
        gain = w_norm.astype(F32).reshape(1, d_model)
        w_kv = jnp.concatenate([w_k, w_v], axis=1)

        nb = 4

        def rows_spec(n, w):
            return pl.BlockSpec((n, seq, w), lambda i: (i, 0, 0))

        def full(*shape):
            return pl.BlockSpec(shape, lambda i: (0,) * len(shape))

        xn, q, kv = pl.pallas_call(
            functools.partial(pre_kernel, scale=scale),
            grid=(batch // nb,),
            in_specs=[rows_spec(nb, d_model), full(1, d_model), full(d_model, width), full(d_model, 2 * hd),
                      full(seq, hd), full(seq, hd)],
            out_specs=[rows_spec(nb, d_model), rows_spec(nb, width), rows_spec(nb, 2 * hd)],
            out_shape=[jax.ShapeDtypeStruct((batch, seq, d_model), BF16),
                       jax.ShapeDtypeStruct((batch, seq, width), BF16),
                       jax.ShapeDtypeStruct((batch, seq, 2 * hd), BF16)],
            compiler_params=pltpu.CompilerParams(vmem_limit_bytes=VMEM_LIMIT),
            cost_estimate=pl.CostEstimate(flops=2 * tokens * d_model * (width + 2 * hd),
                                          bytes_accessed=6 * tokens * d_model, transcendentals=0),
            name='project',
        )(x, gain, w_q, w_kv, cos2, sin2)

        kv_all = lax.all_gather(kv, 'sp', axis=0, tiled=False)
        d_o = jnp.einsum('bsd,ed->bse', dy, w_o, preferred_element_type=F32).astype(BF16)

        last = batch - 1
        steps = batch + 3
        f32_tile = (seq, hd)
        o, dq, dkv = pl.pallas_call(
            functools.partial(attention_kernel, batch, scale=scale),
            grid=(steps,),
            in_specs=[pl.BlockSpec((1, 8, hd), lambda i: (jnp.minimum(i, last), 0, 0)),
                      pl.BlockSpec((1, seq, width), lambda i: (jnp.minimum(i, last), 0, 0)),
                      pl.BlockSpec((1, seq, width), lambda i: (jnp.minimum(i, last), 0, 0)),
                      pl.BlockSpec((groups, 1, seq, 2 * hd), lambda i: (0, jnp.minimum(i, last), 0, 0)),
                      full(seq, hd), full(seq, hd)],
            out_specs=[pl.BlockSpec((1, seq, width), lambda i: (jnp.minimum(i, last), 0, 0)),
                       pl.BlockSpec((1, seq, width), lambda i: (jnp.minimum(i, last), 0, 0)),
                       pl.BlockSpec((1, seq, 2 * hd), lambda i: (jnp.maximum(i - 3, 0), 0, 0))],
            out_shape=[jax.ShapeDtypeStruct((batch, seq, width), BF16),
                       jax.ShapeDtypeStruct((batch, seq, width), BF16),
                       jax.ShapeDtypeStruct((batch, seq, 2 * hd), F32)],
            scratch_shapes=[
                pltpu.VMEM((2, keys, 2 * hd), F32), pltpu.VMEM((2, keys, 2 * hd), F32), pltpu.VMEM((2, keys, 2 * hd), F32),
                pltpu.VMEM((keys, 2 * hd), BF16), pltpu.VMEM((keys, hd), BF16),
                pltpu.VMEM((hd, keys), BF16), pltpu.VMEM((hd, keys), BF16),
                pltpu.VMEM((seq, seq), BF16), pltpu.VMEM((2, 8, 2 * hd), F32), pltpu.VMEM((2, 8, 2 * hd), F32),
                pltpu.VMEM((2, 2, 4, 2) + f32_tile, F32), pltpu.VMEM((2, 4, 2) + f32_tile, F32),
                pltpu.VMEM((2, 2, 2, 2) + f32_tile, F32), pltpu.VMEM((2, 2, 2) + f32_tile, F32),
                pltpu.VMEM((2, 2, 2) + f32_tile, F32), pltpu.VMEM((2, 2) + f32_tile, F32),
            ] + [pltpu.SemaphoreType.DMA((2,))] * 6 + [pltpu.SemaphoreType.REGULAR((2,))] * 3,
            compiler_params=pltpu.CompilerParams(vmem_limit_bytes=VMEM_LIMIT, collective_id=0, has_side_effects=True),
            cost_estimate=pl.CostEstimate(flops=12 * tokens * width * keys, bytes_accessed=12 * tokens * width,
                                          transcendentals=tokens * width // hd * keys),
            name='attend',
        )(jnp.broadcast_to(prefix_len[:, None, None], (batch, 8, hd)), q, d_o, kv_all, cos2, sin2)

        d_wo = jnp.einsum('bse,bsd->ed', o, dy, preferred_element_type=F32)
        d_wo, xn = lax.optimization_barrier((d_wo, xn))
        d_wo = lax.psum(d_wo, 'sp', axis_index_groups=[[m ^ 1 for m in range(groups)]])

        rot = dkv[..., :hd].astype(BF16).astype(F32)
        rolled = jnp.concatenate([rot[..., half:], rot[..., :half]], axis=-1)
        dk_proj = (rot * cos2 - rolled * sin2).astype(BF16)
        dkv_proj = jnp.concatenate([dk_proj, dkv[..., hd:].astype(BF16)], axis=-1)
        d_wq = jnp.einsum('bsd,bse->de', xn, dq, preferred_element_type=F32)
        d_wkv = jnp.einsum('bsd,bse->de', xn, dkv_proj, preferred_element_type=F32)
        d_wq, d_wkv, o, dq = lax.optimization_barrier((d_wq, d_wkv, o, dq))
        d_wq, d_wkv = lax.psum((d_wq, d_wkv), 'sp')

        mixed = jnp.einsum('bse,ed->bsd', o, w_o, preferred_element_type=F32)
        y = (x.astype(F32) + mixed).astype(BF16)

        nb2 = 2
        dx, dgain = pl.pallas_call(
            post_kernel,
            grid=(batch // nb2,),
            in_specs=[rows_spec(nb2, width), rows_spec(nb2, 2 * hd), full(d_model, width), full(d_model, 2 * hd),
                      rows_spec(nb2, d_model), rows_spec(nb2, d_model), full(1, d_model)],
            out_specs=[rows_spec(nb2, d_model), full(8, d_model)],
            out_shape=[jax.ShapeDtypeStruct((batch, seq, d_model), BF16), jax.ShapeDtypeStruct((8, d_model), F32)],
            compiler_params=pltpu.CompilerParams(vmem_limit_bytes=VMEM_LIMIT),
            cost_estimate=pl.CostEstimate(flops=2 * tokens * d_model * (width + 2 * hd),
                                          bytes_accessed=8 * tokens * d_model, transcendentals=0),
            name='norm_grad',
        )(dq, dkv_proj, w_q, w_kv, x, dy, gain)
        d_gain = lax.psum(jnp.sum(dgain, axis=0), 'sp')
        return y, dx, d_wq, d_wkv[:, :hd], d_wkv[:, hd:], d_wo, d_gain

    return jax.shard_map(local_block, mesh=mesh, in_specs=(seq_spec, seq_spec, whole, whole, whole, whole, whole, whole), out_specs=(seq_spec, seq_spec, whole, whole, whole, whole, whole), check_vma=False)
```

time: 3420 us -> 1030 us (0.30)
  matrix products: 1370 us -> 183 us
  other arithmetic: 1000 us -> 10.8 us
  Pallas kernels: 0 us -> 407 us
  waiting for transfers between devices: 739 us -> 349 us
  local copies, waits for them, and re-layouts: 225 us -> 32.7 us
    dot_general x68 -> x5, matrix products: 1370 us -> 183 us  [the longest x1 44.1 us: local_block(): d_wo = jnp.einsum('bse,bsd->ed', o, dy, preferred_element_type=F32)]
    sub x17 -> x0, other arithmetic: 650 us -> none  [the longest x8 317 us: attend_forward(): jax.nn.softmax(jnp.where(visible, scores, MASK_FILL), axis=-1)]
    all_to_all x4 -> x0, waiting for transfers between devices: 470 us -> none  [the longest x1 168 us: local_block(): q_heads = lax.all_to_all(q_send, 'sp', 0, 0, tiled=True)]
    pallas_call x0 -> x3, Pallas kernels: none -> 407 us  [the longest x1 293 us: local_block(): pl.pallas_call(functools.partial(attention_kernel, batch, scale=scale), g...]
    convert_element_type x12 -> x3, other arithmetic: 222 us -> 3.34 us  [the longest x1 2.93 us: local_block(): dk_proj = (rot * cos2 - rolled * sin2).astype(BF16)]
    or x16 -> x0, other arithmetic: 70.8 us -> none  [visible_mask(): (key_grid < prefix_len[:, None, None, None]) | (key_grid <= query_pos[Non...]
    reshape x3 -> x0, local copies, waits for them, and re-layouts: 52.9 us -> none  [the longest x2 35.3 us: local_block(): w_q4 = w_q.reshape(d_model, groups, local_heads, head_dim)]
    dynamic_slice x32 -> x0, local copies, waits for them, and re-layouts: 45.1 us -> none  [local_block(): o_heads = lax.map(forward_block, (q_heads, block_ids))]
  transfers between devices with their start and end apart: 9 -> 3, of which waited for: 4 -> 3; matrix products, arithmetic and copies ran while one was open for 34% -> 9% of each run, Pallas kernels for 0% -> 6%
where the time goes in v1:
time: 1030 us; the launch traced here: 1020 us
  Pallas kernels  407 us (40%)
  waiting for transfers between devices  349 us (34%)
  matrix products  183 us (18%)
  local copies, waits for them, and re-layouts  32.7 us (3%)
  blocking collectives  23.9 us (2%)
  between operations  14.1 us (1%)
  other arithmetic  10.8 us (1%)
    pallas_call x1, Pallas kernels, local_block(): pl.pallas_call(functools.partial(attention_kernel, batch, scale=scale), g...  293 us
    psum x1, waiting for transfers between devices, local_block(): lax.psum(d_wo, 'sp', axis_index_groups=[[m ^ 1 for m in range(groups)]])  208 us
    psum x1, waiting for transfers between devices, local_block(): d_wq, d_wkv = lax.psum((d_wq, d_wkv), 'sp')  96.3 us
    pallas_call x1, Pallas kernels, local_block(): pl.pallas_call(post_kernel, grid=(batch // nb2,), in_specs=[rows_spec(nb2...  61.9 us
    pallas_call x1, Pallas kernels, local_block(): pl.pallas_call(functools.partial(pre_kernel, scale=scale), grid=(batch //...  51.5 us
    all_gather x1, waiting for transfers between devices, local_block(): kv_all = lax.all_gather(kv, 'sp', axis=0, tiled=False)  45.1 us
    dot_general x1, matrix products, local_block(): d_wo = jnp.einsum('bse,bsd->ed', o, dy, preferred_element_type=F32)  44.1 us
    dot_general x1, matrix products, local_block(): d_wq = jnp.einsum('bsd,bse->de', xn, dq, preferred_element_type=F32)  44 us
  transfers between devices with their start and end apart: 3, of which 3 were waited for; matrix products, arithmetic and copies ran while one was open for 9% of the time, Pallas kernels for 6%

profile of v1, /device:TPU:0, one launch (start us, length us, event | category | flops | bytes accessed | tf_op | source)
XLA Modules:
  0.0 1020.7 jit_solution(18362903525561364644)
XLA Ops:
  7.2 1.3 reshape.34
  8.5 1.1 constant_dynamic-update-slice_fusion.1
  10.0 1.2 constant_dynamic-update-slice_fusion.wkv_ref
  12.2 51.5 %project.1 = (bf16[32,128,2048]{2,1,0:T(8,128)(2,1)}, bf16[32,128,2048]{2,1,0:T(8,128)(2,1)}, bf16[32,128,256]{2,1,0:T(8,128)(2,1)}) custom-call(bf16[32,128,2048]{2,1,0:T(8,128)(2,1)} %x_ref.3, f32[1,2048]{1,0:T(1,128)} %bitcast.20, bf16[2048,2048]{1,0:T(8,128)(2,1)} %wq_ref.3, bf16[2048,256]{1,0:T(8,128)(2,1)} %copy-done.5, ...), custom_call_target="tpu_custom_call" | custom-call | flops 38654705664 | bytes 50331648 | tf_op jit(solution)/shard_map/project/pallas_call | solution.py:314
  64.1 41.7 %convolution_convert_fusion.do_ref = bf16[32,128,2048]{2,1,0:T(8,128)(2,1)} fusion(bf16[32,128,2048]{2,1,0:T(8,128)(2,1)} %dy_ref.1, bf16[2048,2048]{1,0:T(8,128)(2,1)} %param.15), kind=kOutput, calls=%fused_computation.1 | convolution fusion | flops 34368126976 | bytes 41943040 | tf_op jit(solution)/shard_map/bsd,ed->bse/dot_general | solution.py:330
  105.8 45.1 %all-gather.3.cloned.1.call-done = bf16[256,128,256]{2,1,0:T(8,128)(2,1)} async-done(((bf16[32,128,256]{2,1,0:T(8,128)(2,1)}), bf16[256,128,256]{2,1,0:T(8,128)(2,1)}) %all-gather.3.cloned.1.call-update) | async-done | bytes 16777232 | tf_op jit(solution)/shard_map/all_gather | solution.py:329
  151.6 293.5 %attend.1 = (bf16[32,128,2048]{2,1,0:T(8,128)(2,1)}, bf16[32,128,2048]{2,1,0:T(8,128)(2,1)}, f32[32,128,256]{2,1,0:T(8,128)}) custom-call(s32[32,8,128]{2,1,0:T(8,128)} %broadcast_in_dim.2.prefix_ref, bf16[32,128,2048]{2,1,0:T(8,128)(2,1)} %get-tuple-element.21.q_ref, bf16[32,128,2048]{2,1,0:T(8,128)(2,1)} %convolution_convert_fusion.do_ref, ...), custom_call_target="tpu_custom_call" | custom-call | flops 103079215104 | bytes 100663296 | tf_op jit(solution)/shard_map/attend/pallas_call | solution.py:335
  445.1 2.5 convert.5
  448.0 2.7 fusion.6
  450.7 44.1 %convolution_bitcast_fusion.1 = f32[2048,2048]{1,0:T(8,128)} fusion(bf16[32,128,2048]{2,1,0:T(8,128)(2,1)} %get-tuple-element.28, bf16[32,128,2048]{2,1,0:T(8,128)(2,1)} %dy_ref.1), kind=kOutput, calls=%fused_computation.3 | convolution fusion | flops 34359738368 | bytes 50331648 | tf_op jit(solution)/shard_map/bse,bsd->ed/dot_general | solution.py:364
  494.9 2.9 fusion.3
  497.8 44.0 %convolution_bitcast_fusion = f32[2048,2048]{1,0:T(8,128)} fusion(bf16[32,128,2048]{2,1,0:T(8,128)(2,1)} %get-tuple-element.25, bf16[32,128,2048]{2,1,0:T(8,128)(2,1)} %get-tuple-element.29.dq_ref), kind=kOutput, calls=%fused_computation.2 | convolution fusion | flops 34359738368 | bytes 50331648 | tf_op jit(solution)/shard_map/bsd,bse->de/dot_general | solution.py:372
  541.8 9.7 convolution_bitcast_fusion.2
  551.6 1.1 copy-done.2
  552.8 1.6 pad_maximum_fusion.dkv_ref
  554.4 61.9 %norm_grad.1 = (bf16[32,128,2048]{2,1,0:T(8,128)(2,1)}, f32[8,2048]{1,0:T(8,128)}) custom-call(bf16[32,128,2048]{2,1,0:T(8,128)(2,1)} %get-tuple-element.29.dq_ref, bf16[32,128,256]{2,1,0:T(8,128)(2,1)} %pad_maximum_fusion.dkv_ref, bf16[2048,2048]{1,0:T(8,128)(2,1)} %wq_ref.3, bf16[2048,256]{1,0:T(8,128)(2,1)} %copy-done.5, bf16[32,128,2048]{2,1,0:T(8,128)(2,1)} %x_ref.3, ...), custom_call_target="tpu_custom_call" | custom-call | flops 38654705664 | bytes 67108864 | tf_op jit(solution)/shard_map/norm_grad/pallas_call | solution.py:381
  617.2 23.9 %psum.31 = f32[2048]{0:T(1024)} all-reduce(f32[2048]{0:T(1024)S(1)} %reduce_sum.9), channel_id=1, replica_groups=mesh['sp'=8] {'sp'}, use_global_device_ids=true, to_apply=%region_4.0 | all-reduce | flops 2048 | bytes 16384 | tf_op jit(solution)/shard_map/psum | solution.py:393
  641.1 43.5 %add_convert_fusion = bf16[32,128,2048]{2,1,0:T(8,128)(2,1)} fusion(bf16[32,128,2048]{2,1,0:T(8,128)(2,1)} %x_ref.3, bf16[32,128,2048]{2,1,0:T(8,128)(2,1)} %get-tuple-element.28, bf16[2048,2048]{1,0:T(8,128)(2,1)} %param.15), kind=kOutput, calls=%fused_computation | convolution fusion | flops 34384904192 | bytes 58720256 | tf_op jit(solution)/shard_map/bse,ed->bsd/dot_general | solution.py:377
  684.6 96.3 %all-reduce.6.cloned.1.call-done = (f32[2048,2048]{1,0:T(8,128)}, f32[2048,256]{1,0:T(8,128)}) async-done(((f32[2048,2048]{1,0:T(8,128)}, f32[2048,256]{1,0:T(8,128)}), (f32[2048,2048]{1,0:T(8,128)}, f32[2048,256]{1,0:T(8,128)})) %all-reduce.6.cloned.1.call-update) | async-done | bytes 18874384 | tf_op jit(solution)/shard_map/psum | solution.py:375
  780.8 3.0 fusion.5
  783.8 207.5 %all-reduce.4.cloned.1.call-done = f32[2048,2048]{1,0:T(8,128)} async-done(((f32[2048,2048]{1,0:T(8,128)}), f32[2048,2048]{1,0:T(8,128)}) %all-reduce.4.cloned.1.call-update) | async-done | bytes 16777232 | tf_op jit(solution)/shard_map/psum | solution.py:366
  991.4 12.7 %copy.28 = f32[2048,2048]{1,0:T(8,128)} copy(f32[2048,2048]{1,0:T(8,128)} %get-tuple-element.50) | data formatting | bytes 33554432
  1004.0 3.7 copy-done
  1007.8 6.2 copy.29
  (25 shorter events, 3.8 us)
Async XLA Ops:
  7.2 143.7 %all-gather.3.cloned.1.call-start = ((), (), s32[]{:S(2)}) async-start(), calls=%async_computation.1 | async-start | bytes 18874368 | tf_op jit(solution)/shard_map/all_gather | solution.py:329
  11.2 1.0 copy-start.5
  63.7 87.1 %copy-start.6 = (s32[32]{0:T(128)S(1)}, s32[32]{0:T(128)}, u32[]{:S(2)}) copy-start(s32[32]{0:T(128)} %param.10) | copy-start | bytes 388
  63.7 717.1 %all-reduce.6.cloned.1.call-start = ((), (), s32[]{:S(2)}) async-start(), calls=%async_computation.2 | async-start | bytes 37748736 | tf_op jit(solution)/shard_map/psum | solution.py:375
  450.7 44.1 %copy-start.3 = (f32[128,128]{1,0:T(8,128)S(1)}, f32[128,128]{1,0:T(8,128)}, u32[]{:S(2)}) copy-start(f32[128,128]{1,0:T(8,128)} %get-tuple-element.46.cos_ref) | copy-start | bytes 196612
  450.7 44.2 %copy-start.4 = (f32[128,128]{1,0:T(8,128)S(1)}, f32[128,128]{1,0:T(8,128)}, u32[]{:S(2)}) copy-start(f32[128,128]{1,0:T(8,128)} %get-tuple-element.47.sin_ref) | copy-start | bytes 196612
  497.8 44.0 %copy-start.1 = (bf16[32,128,128]{2,1,0:T(8,128)(2,1)}, bf16[32,128,128]{2,1,0:T(8,128)(2,1)S(1)}, u32[]{:S(2)}) copy-start(bf16[32,128,128]{2,1,0:T(8,128)(2,1)S(1)} %fusion.3) | copy-start | bytes 3145732
  551.5 1.2 copy-start.2
  551.6 439.8 %all-reduce.4.cloned.1.call-start = ((), (), s32[]{:S(2)}) async-start(), calls=%async_computation | async-start | bytes 33554432 | tf_op jit(solution)/shard_map/psum | solution.py:366
  991.4 16.4 %copy-start = (f32[2048,2048]{1,0:T(8,128)S(1)}, f32[2048,2048]{1,0:T(8,128)}, u32[]{:S(2)}) copy-start(f32[2048,2048]{1,0:T(8,128)} %all-reduce.4.cloned.1.call-done) | copy-start | bytes 50331652
Sparse Core Ops, SparseCore 0:
  63.8 86.9 all-gather.2
  551.7 229.1 all-reduce.5
  784.6 206.7 all-reduce.3

commit v2 on v1

v2 whole, which is shorter than its diff:
```python
import functools

import jax
import jax.numpy as jnp
from jax import lax
from jax.experimental import pallas as pl
from jax.experimental.pallas import tpu as pltpu
from jax.sharding import PartitionSpec as P


ROPE_THETA = 10000.0
NORM_EPS = 1e-6
MASK_FILL = -1e30
F32 = jnp.float32
BF16 = jnp.bfloat16
MESH = pl.DeviceIdType.MESH
CHUNKS = 4
VMEM_LIMIT = 60 * 1024 * 1024
NT = (((1,), (1,)), ((), ()))


def mm(a, b):
    return jnp.dot(a, b, preferred_element_type=F32)


def mm_nt(a, b):
    return lax.dot_general(a, b, NT, preferred_element_type=F32)


def rotate(v, cos, sin):
    return v * cos + pltpu.roll(v, v.shape[-1] // 2, 1) * sin


def norm_kernel(x_ref, gain_ref, wkv_ref, cos_ref, sin_ref, xn_ref, kv_ref):
    nb, seq, d_model = x_ref.shape
    hd = cos_ref.shape[1]
    rows = nb * seq
    x = x_ref[...].reshape(rows, d_model).astype(F32)
    inv = lax.rsqrt(jnp.mean(x * x, axis=-1, keepdims=True) + NORM_EPS)
    xn = (x * inv * (1.0 + gain_ref[...])).astype(BF16)
    xn_ref[...] = xn.reshape(nb, seq, d_model)
    cos = jnp.concatenate([cos_ref[...]] * nb, axis=0)
    sin = jnp.concatenate([sin_ref[...]] * nb, axis=0)
    kv = mm(xn, wkv_ref[...])
    kv_ref[:, :, :hd] = rotate(kv[:, :hd], cos, sin).astype(BF16).reshape(nb, seq, hd)
    kv_ref[:, :, hd:] = kv[:, hd:].astype(BF16).reshape(nb, seq, hd)


def query_kernel(xn_ref, wq_ref, cos_ref, sin_ref, q_ref, *, scale):
    nb, seq, d_model = xn_ref.shape
    hd = cos_ref.shape[1]
    xn = xn_ref[...].reshape(nb * seq, d_model)
    cos = jnp.concatenate([cos_ref[...]] * nb, axis=0)
    sin = jnp.concatenate([sin_ref[...]] * nb, axis=0)
    width = wq_ref.shape[1]
    step = 512
    for n in range(width // step):
        proj = mm(xn, wq_ref[:, n * step:(n + 1) * step])
        for h in range(step // hd):
            rot = rotate(proj[:, h * hd:(h + 1) * hd], cos, sin) * scale
            lo = n * step + h * hd
            q_ref[:, :, lo:lo + hd] = rot.astype(BF16).reshape(nb, seq, hd)


def attention_kernel(batch, first, last, *refs, scale):
    refs = list(refs)
    prefix_ref, q_ref, do_ref, q_was, do_was, kv_ref, cos_ref, sin_ref = refs[:8]
    del refs[:8]
    carry_ref = None if first else refs.pop(0)
    o_ref, dq_ref, dkv_ref = refs[:3]
    s_scr, e_scr, dp_scr, k_ext, v_scr, k_t, v_t, eye_scr, top_scr, stat_scr = refs[3:13]
    if last:
        (part, recv1, sum1, recv2, sum2, recv3,
         send1, got1, send2, got2, send3, got3, free1, free2, free3) = refs[13:]
    t = pl.program_id(0)
    me = lax.axis_index('sp')
    core = me % 2
    x_bit = (me // 2) % 2
    y_bit = me // 4
    partner = me + 1 - 2 * core
    x_near = me + 2 - 4 * x_bit
    y_near = me + 4 - 8 * y_bit
    near_1 = x_near * (1 - core) + y_near * core
    near_2 = y_near * (1 - core) + x_near * core
    bit_1 = x_bit * (1 - core) + y_bit * core
    bit_2 = y_bit * (1 - core) + x_bit * core

    groups, _, seq, _ = kv_ref.shape
    hd = kv_ref.shape[3] // 2
    keys = groups * seq
    chunk = 256

    def copy_1(slot):
        return pltpu.make_async_remote_copy(part.at[slot, 1 - core], recv1.at[slot], send1.at[slot], got1.at[slot],
                                            device_id=(partner,), device_id_type=MESH)

    def copy_2(slot):
        return pltpu.make_async_remote_copy(sum1.at[slot, 1 - bit_1], recv2.at[slot], send2.at[slot], got2.at[slot],
                                            device_id=(near_1,), device_id_type=MESH)

    def copy_3(slot):
        return pltpu.make_async_remote_copy(sum2.at[slot, 1 - bit_2], recv3.at[slot], send3.at[slot], got3.at[slot],
                                            device_id=(near_2,), device_id_type=MESH)

    if last:
        @pl.when(t == 0)
        def _():
            barrier = pltpu.get_barrier_semaphore()
            for other in (partner, near_1, near_2):
                pl.semaphore_signal(barrier, inc=1, device_id=(other,), device_id_type=MESH)
            pl.semaphore_wait(barrier, 3)

    @pl.when(t == 0)
    def _():
        eye_scr[...] = (lax.broadcasted_iota(jnp.int32, (seq, seq), 0)
                        == lax.broadcasted_iota(jnp.int32, (seq, seq), 1)).astype(F32).astype(BF16)

    def fold(a, op):
        return op(a.reshape(chunk // 8, 8, 2 * hd), axis=0)

    def heads_of(ref, lo):
        return jnp.concatenate([ref[0, :, pl.ds(lo, hd)], ref[0, :, pl.ds(lo + hd, hd)]], axis=0)

    def masked_q(lo):
        eye = eye_scr[...]
        return jnp.concatenate([heads_of(q_ref, lo), jnp.concatenate([eye, eye], axis=0)], axis=1)

    low = functools.partial(jnp.full, (8, 2 * hd), MASK_FILL, F32)

    @pl.when(t <= batch)
    def _():
        now, was = t % 2, (t + 1) % 2
        k_all = kv_ref[:, 0, :, :hd].reshape(keys, hd)
        v_all = kv_ref[:, 0, :, hd:].reshape(keys, hd)
        limit = jnp.maximum(prefix_ref[0, 0:1, :], me * seq + lax.broadcasted_iota(jnp.int32, (keys, seq), 1) + 1)
        k_ext[:, :hd] = k_all
        k_ext[:, hd:] = jnp.where(lax.broadcasted_iota(jnp.int32, (keys, seq), 0) < limit, 0.0, MASK_FILL).astype(BF16)
        v_scr[now] = v_all
        k_t[now] = k_all.T
        v_t[now] = v_all.T
        acc = part.at[was] if last else dkv_ref.at[0]
        acc[...] = jnp.zeros(acc.shape, F32) if first else carry_ref[0]

        def score_step(i):
            buf = i
            q_ext = masked_q(i * 2 * hd)
            top = low()
            for c in range(keys // chunk):
                at = slice(c * chunk, (c + 1) * chunk)
                s = mm_nt(k_ext[at, :], q_ext)
                s_scr[buf, at, :] = s
                top = jnp.maximum(top, fold(s, jnp.max))
            top_scr[buf] = top

        def weigh_step(i, source, v_slot):
            buf = i
            do2 = heads_of(source, i * 2 * hd)
            top = jnp.max(top_scr[buf], axis=0, keepdims=True)
            total = jnp.zeros((8, 2 * hd), F32)
            cross = jnp.zeros((8, 2 * hd), F32)
            for c in range(keys // chunk):
                at = slice(c * chunk, (c + 1) * chunk)
                dp = mm_nt(v_scr[v_slot, at, :], do2).astype(BF16).astype(F32)
                e = jnp.exp(s_scr[buf, at, :] - top)
                e_scr[buf, at, :] = e
                dp_scr[buf, at, :] = dp
                total = total + fold(e, jnp.sum)
                cross = cross + fold(e * dp, jnp.sum)
            inv = 1.0 / jnp.sum(total, axis=0, keepdims=True)
            stat_scr[buf, 0:1, :] = inv
            stat_scr[buf, 1:2, :] = jnp.sum(cross, axis=0, keepdims=True) * inv

        def grad_step(i):
            buf = i
            lo = i * 2 * hd
            q2 = heads_of(q_was, lo)
            do2 = heads_of(do_was, lo)
            inv = stat_scr[buf, 0:1, :]
            delta = stat_scr[buf, 1:2, :]
            ps, dss = [], []
            for c in range(keys // chunk):
                at = slice(c * chunk, (c + 1) * chunk)
                p = e_scr[buf, at, :] * inv
                ds = (p * (dp_scr[buf, at, :] - delta)).astype(BF16)
                p = p.astype(BF16)
                ps.append(p)
                dss.append(ds)
                dk = mm(ds, q2)
                dv = mm(p, do2)
                for r in range(chunk // seq):
                    j = c * (chunk // seq) + r
                    acc[j % 2, j // 2, 0] += dk[r * seq:(r + 1) * seq, :]
                    acc[j % 2, j // 2, 1] += dv[r * seq:(r + 1) * seq, :]
            o_t = mm(v_t[was], jnp.concatenate(ps, axis=0)).astype(BF16)
            dq_t = mm(k_t[was], jnp.concatenate(dss, axis=0)).astype(BF16)
            for half in range(2):
                o_ref[0, :, pl.ds(lo + half * hd, hd)] = o_t[:, half * hd:(half + 1) * hd].T
                dq = dq_t[:, half * hd:(half + 1) * hd].T.astype(F32) * scale
                dq_ref[0, :, pl.ds(lo + half * hd, hd)] = rotate(dq, cos_ref[...], -sin_ref[...]).astype(BF16)

        score_step(0)
        weigh_step(1, do_was, was)
        grad_step(0)
        score_step(1)
        weigh_step(0, do_ref, now)
        grad_step(1)

    if not last:
        return

    @pl.when(t >= 4)
    def _():
        slot = t % 2
        copy_3(slot).wait()
        done = sum2[slot, bit_2] + recv3[slot]
        dkv_ref[0, :, :hd] = done[0]
        dkv_ref[0, :, hd:] = done[1]

        @pl.when(t - 4 < batch - 2)
        def _():
            pl.semaphore_signal(free3.at[slot], inc=1, device_id=(near_2,), device_id_type=MESH)

    @pl.when((t >= 3) & (t - 3 < batch))
    def _():
        slot = (t + 1) % 2
        copy_2(slot).wait()
        for s in range(2):
            sum2[slot, s] = sum1[slot, bit_1, s] + recv2[slot, s]

        @pl.when(t - 3 < batch - 2)
        def _():
            pl.semaphore_signal(free2.at[slot], inc=1, device_id=(near_1,), device_id_type=MESH)

        @pl.when(t - 3 >= 2)
        def _():
            pl.semaphore_wait(free3.at[slot], 1)

        copy_3(slot).start()

    @pl.when((t >= 2) & (t - 2 < batch))
    def _():
        slot = t % 2
        copy_1(slot).wait()
        for f in range(2):
            for s in range(2):
                chip = f * (1 + core) + s * (2 - core)
                sum1[slot, f, s] = part[slot, core, chip] + recv1[slot, chip]

        @pl.when(t - 2 < batch - 2)
        def _():
            pl.semaphore_signal(free1.at[slot], inc=1, device_id=(partner,), device_id_type=MESH)

        @pl.when(t - 2 >= 2)
        def _():
            pl.semaphore_wait(free2.at[slot], 1)

        copy_2(slot).start()

    @pl.when((t >= 1) & (t - 1 < batch))
    def _():
        slot = (t + 1) % 2

        @pl.when(t - 1 >= 2)
        def _():
            pl.semaphore_wait(free1.at[slot], 1)

        copy_1(slot).start()


def out_kernel(*refs):
    *o_refs, wo_ref, x_ref, y_ref = refs
    nb, seq, d_model = x_ref.shape
    rows = nb * seq
    o = jnp.concatenate([r[...].reshape(rows, r.shape[2]) for r in o_refs], axis=1)
    step = 512
    for n in range(d_model // step):
        at = slice(n * step, (n + 1) * step)
        x = x_ref[:, :, at].reshape(rows, step).astype(F32)
        y_ref[:, :, at] = (x + mm(o, wo_ref[:, at])).astype(BF16).reshape(nb, seq, step)


def post_kernel(*refs):
    *dq_refs, dkv_ref, wq_ref, wkv_ref, x_ref, dy_ref, gain_ref, dx_ref, dgain_ref = refs
    nb, seq, d_model = x_ref.shape
    rows = nb * seq
    dq = jnp.concatenate([r[...].reshape(rows, r.shape[2]) for r in dq_refs], axis=1)
    acc = mm_nt(dq, wq_ref[...])
    acc = acc + mm_nt(dkv_ref[...].reshape(rows, dkv_ref.shape[2]), wkv_ref[...])
    g = acc.astype(BF16).astype(F32)
    x = x_ref[...].reshape(rows, d_model).astype(F32)
    inv = lax.rsqrt(jnp.mean(x * x, axis=-1, keepdims=True) + NORM_EPS)
    xr = x * inv
    part = jnp.sum((g * xr).reshape(rows // 8, 8, d_model), axis=0)
    u = g * (1.0 + gain_ref[...])
    mean = jnp.mean(u * xr, axis=-1, keepdims=True)
    dy = dy_ref[...].reshape(rows, d_model).astype(F32)
    dx_ref[...] = (dy + inv * (u - xr * mean)).astype(BF16).reshape(nb, seq, d_model)

    @pl.when(pl.program_id(0) == 0)
    def _():
        dgain_ref[...] = jnp.zeros_like(dgain_ref)

    dgain_ref[...] += part


def solution(mesh):
    groups = mesh.shape['sp']
    seq_spec = P(None, 'sp', None)
    whole = P()

    def local_block(x, dy, prefix_len, w_norm, w_q, w_k, w_v, w_o):
        batch, seq, d_model = x.shape
        hd = w_k.shape[1]
        width = w_q.shape[1]
        keys = seq * groups
        tokens = batch * seq
        scale = hd ** -0.5
        me = lax.axis_index('sp')
        half = hd // 2
        freq = ROPE_THETA ** (-2.0 * jnp.arange(half, dtype=F32) / hd)
        angles = (me * seq + jnp.arange(seq)).astype(F32)[:, None] * freq[None, :]
        cos, sin = jnp.cos(angles), jnp.sin(angles)
        cos2 = jnp.concatenate([cos, cos], axis=1)
        sin2 = jnp.concatenate([-sin, sin], axis=1)
        gain = w_norm.astype(F32).reshape(1, d_model)
        w_kv = jnp.concatenate([w_k, w_v], axis=1)

        nb = 4

        def rows_spec(n, w):
            return pl.BlockSpec((n, seq, w), lambda i: (i, 0, 0))

        def full(*shape):
            return pl.BlockSpec(shape, lambda i: (0,) * len(shape))

        xn, kv = pl.pallas_call(
            norm_kernel,
            grid=(batch // nb,),
            in_specs=[rows_spec(nb, d_model), full(1, d_model), full(d_model, 2 * hd), full(seq, hd), full(seq, hd)],
            out_specs=[rows_spec(nb, d_model), rows_spec(nb, 2 * hd)],
            out_shape=[jax.ShapeDtypeStruct((batch, seq, d_model), BF16),
                       jax.ShapeDtypeStruct((batch, seq, 2 * hd), BF16)],
            compiler_params=pltpu.CompilerParams(vmem_limit_bytes=VMEM_LIMIT),
            cost_estimate=pl.CostEstimate(flops=4 * tokens * d_model * hd, bytes_accessed=4 * tokens * d_model,
                                          transcendentals=0),
            name='norm',
        )(x, gain, w_kv, cos2, sin2)
        kv_all = lax.all_gather(kv, 'sp', axis=0, tiled=False)
        q = pl.pallas_call(
            functools.partial(query_kernel, scale=scale),
            grid=(batch // nb,),
            in_specs=[rows_spec(nb, d_model), full(d_model, width), full(seq, hd), full(seq, hd)],
            out_specs=rows_spec(nb, width),
            out_shape=jax.ShapeDtypeStruct((batch, seq, width), BF16),
            compiler_params=pltpu.CompilerParams(vmem_limit_bytes=VMEM_LIMIT),
            cost_estimate=pl.CostEstimate(flops=2 * tokens * d_model * width, bytes_accessed=4 * tokens * d_model,
                                          transcendentals=0),
            name='query',
        )(xn, w_q, cos2, sin2)
        d_o = jnp.einsum('bsd,ed->bse', dy, w_o, preferred_element_type=F32).astype(BF16)

        end = batch - 1
        f32_tile = (seq, hd)
        prefix = jnp.broadcast_to(prefix_len[:, None, None], (batch, 8, hd))
        cols = width // CHUNKS
        split = (2, groups // 2, 2) + f32_tile

        def attend(n, q, d_o, carry):
            first, last = n == 0, n == CHUNKS - 1
            before = lambda i: jnp.clip(i - 1, 0, end)
            here = lambda i: (before(i), 0, 0)
            part_spec = pl.BlockSpec((1,) + split, lambda i: (before(i), 0, 0, 0, 0, 0))
            in_specs = [pl.BlockSpec((1, 8, hd), lambda i: (jnp.minimum(i, end), 0, 0)),
                        pl.BlockSpec((1, seq, cols), lambda i: (jnp.minimum(i, end), 0, n)),
                        pl.BlockSpec((1, seq, cols), lambda i: (jnp.minimum(i, end), 0, n)),
                        pl.BlockSpec((1, seq, cols), lambda i: (before(i), 0, n)),
                        pl.BlockSpec((1, seq, cols), lambda i: (before(i), 0, n)),
                        pl.BlockSpec((groups, 1, seq, 2 * hd), lambda i: (0, jnp.minimum(i, end), 0, 0)),
                        full(seq, hd), full(seq, hd)]
            args = [prefix, q, d_o, q, d_o, kv_all, cos2, sin2]
            if not first:
                in_specs.append(part_spec)
                args.append(carry)
            scratch = [
                pltpu.VMEM((2, keys, 2 * hd), F32), pltpu.VMEM((2, keys, 2 * hd), F32), pltpu.VMEM((2, keys, 2 * hd), F32),
                pltpu.VMEM((keys, 2 * hd), BF16), pltpu.VMEM((2, keys, hd), BF16),
                pltpu.VMEM((2, hd, keys), BF16), pltpu.VMEM((2, hd, keys), BF16),
                pltpu.VMEM((seq, seq), BF16), pltpu.VMEM((2, 8, 2 * hd), F32), pltpu.VMEM((2, 8, 2 * hd), F32)]
            params = dict(vmem_limit_bytes=VMEM_LIMIT)
            if last:
                dkv_spec = pl.BlockSpec((1, seq, 2 * hd), lambda i: (jnp.maximum(i - 4, 0), 0, 0))
                dkv_shape = jax.ShapeDtypeStruct((batch, seq, 2 * hd), F32)
                scratch += [pltpu.VMEM((2,) + split, F32), pltpu.VMEM((2, 4, 2) + f32_tile, F32),
                            pltpu.VMEM((2, 2, 2, 2) + f32_tile, F32), pltpu.VMEM((2, 2, 2) + f32_tile, F32),
                            pltpu.VMEM((2, 2, 2) + f32_tile, F32), pltpu.VMEM((2, 2) + f32_tile, F32)]
                scratch += [pltpu.SemaphoreType.DMA((2,))] * 6 + [pltpu.SemaphoreType.REGULAR((2,))] * 3
                params.update(collective_id=0, has_side_effects=True)
            else:
                dkv_spec = part_spec
                dkv_shape = jax.ShapeDtypeStruct((batch,) + split, F32)
            return pl.pallas_call(
                functools.partial(attention_kernel, batch, first, last, scale=scale),
                grid=(batch + 1 + 3 * last,),
                in_specs=in_specs,
                out_specs=[pl.BlockSpec((1, seq, cols), here), pl.BlockSpec((1, seq, cols), here), dkv_spec],
                out_shape=[jax.ShapeDtypeStruct((batch, seq, cols), BF16),
                           jax.ShapeDtypeStruct((batch, seq, cols), BF16), dkv_shape],
                scratch_shapes=scratch,
                compiler_params=pltpu.CompilerParams(**params),
                cost_estimate=pl.CostEstimate(flops=12 * tokens * cols * keys, bytes_accessed=12 * tokens * cols,
                                              transcendentals=tokens * cols // hd * keys),
                name='attend',
            )(*args)

        os, dqs, d_wos, d_wqs = [], [], [], []
        carry = None
        for n in range(CHUNKS):
            o, dq, carry = attend(n, q, d_o, carry)
            os.append(o)
            dqs.append(dq)
            d_wo = jnp.einsum('bse,bsd->ed', o, dy, preferred_element_type=F32)
            d_wq = jnp.einsum('bsd,bse->de', xn, dq, preferred_element_type=F32)
            if n < CHUNKS - 1:
                d_wo, d_wq, q, carry = lax.optimization_barrier((d_wo, d_wq, q, carry))
                order = [m ^ (n + 1) for m in range(groups)]
                d_wo, d_wq = lax.psum((d_wo, d_wq), 'sp', axis_index_groups=[order])
            else:
                dkv = carry
                rot = dkv[..., :hd].astype(BF16).astype(F32)
                rolled = jnp.concatenate([rot[..., half:], rot[..., :half]], axis=-1)
                dk_proj = (rot * cos2 - rolled * sin2).astype(BF16)
                dkv_proj = jnp.concatenate([dk_proj, dkv[..., hd:].astype(BF16)], axis=-1)
                d_wkv = jnp.einsum('bsd,bse->de', xn, dkv_proj, preferred_element_type=F32)
                d_wo, d_wq, d_wkv, x_b, dy_b = lax.optimization_barrier((d_wo, d_wq, d_wkv, x, dy))
                d_wo, d_wq, d_wkv = lax.psum((d_wo, d_wq, d_wkv), 'sp')
            d_wos.append(d_wo)
            d_wqs.append(d_wq)
        d_wo = jnp.concatenate(d_wos, axis=0)
        d_wq = jnp.concatenate(d_wqs, axis=1)

        nb2 = 2
        dx, dgain = pl.pallas_call(
            post_kernel,
            grid=(batch // nb2,),
            in_specs=[rows_spec(nb2, cols)] * CHUNKS + [
                rows_spec(nb2, 2 * hd), full(d_model, width), full(d_model, 2 * hd),
                rows_spec(nb2, d_model), rows_spec(nb2, d_model), full(1, d_model)],
            out_specs=[rows_spec(nb2, d_model), full(8, d_model)],
            out_shape=[jax.ShapeDtypeStruct((batch, seq, d_model), BF16), jax.ShapeDtypeStruct((8, d_model), F32)],
            compiler_params=pltpu.CompilerParams(vmem_limit_bytes=VMEM_LIMIT),
            cost_estimate=pl.CostEstimate(flops=2 * tokens * d_model * (width + 2 * hd),
                                          bytes_accessed=8 * tokens * d_model, transcendentals=0),
            name='norm_grad',
        )(*dqs, dkv_proj, w_q, w_kv, x_b, dy_b, gain)
        d_gain = lax.psum(jnp.sum(dgain, axis=0), 'sp')
        y = pl.pallas_call(
            out_kernel,
            grid=(batch // nb,),
            in_specs=[rows_spec(nb, cols)] * CHUNKS + [full(width, d_model), rows_spec(nb, d_model)],
            out_specs=rows_spec(nb, d_model),
            out_shape=jax.ShapeDtypeStruct((batch, seq, d_model), BF16),
            compiler_params=pltpu.CompilerParams(vmem_limit_bytes=VMEM_LIMIT),
            cost_estimate=pl.CostEstimate(flops=2 * tokens * d_model * width, bytes_accessed=6 * tokens * d_model,
                                          transcendentals=0),
            name='output',
        )(*os, w_o, x_b)
        return y, dx, d_wq, d_wkv[:, :hd], d_wkv[:, hd:], d_wo, d_gain


    return jax.shard_map(local_block, mesh=mesh, in_specs=(seq_spec, seq_spec, whole, whole, whole, whole, whole, whole), out_specs=(seq_spec, seq_spec, whole, whole, whole, whole, whole), check_vma=False)
```

time: 1030 us -> 1220 us (1.18)
  Pallas kernels: 407 us -> 606 us
  local copies, waits for them, and re-layouts: 32.7 us -> 10.2 us
  other arithmetic: 10.8 us -> 29.2 us
  matrix products: 183 us -> 166 us
  waiting for transfers between devices: 349 us -> 362 us
    pallas_call x2 -> x7, Pallas kernels: 345 us -> 543 us  [the longest x4 439 us: attend(): pl.pallas_call(functools.partial(attention_kernel, batch, first, last, sc...]
    psum x2 -> x4, waiting for transfers between devices: 304 us -> 359 us  [the longest x3 354 us: local_block(): d_wo, d_wq = lax.psum((d_wo, d_wq), 'sp', axis_index_groups=[order])]
    dot_general x1 -> x0, matrix products: 43.5 us -> none  [local_block(): mixed = jnp.einsum('bse,ed->bsd', o, w_o, preferred_element_type=F32)]
    all_gather x1, waiting for transfers between devices: 45.1 us -> 2.06 us  [local_block(): kv_all = lax.all_gather(kv, 'sp', axis=0, tiled=False)]
    concatenate x0 -> x2, other arithmetic: none -> 20.7 us  [the longest x1 13.4 us: local_block(): d_wq = jnp.concatenate(d_wqs, axis=1)]
    unnamed x17 -> x31, local copies, waits for them, and re-layouts: 25 us -> 4.48 us
    dot_general x1 -> x4, matrix products: 44.1 us -> 57.6 us  [local_block(): d_wo = jnp.einsum('bse,bsd->ed', o, dy, preferred_element_type=F32)]
    dot_general x1 -> x4, matrix products: 44 us -> 57.1 us  [local_block(): d_wq = jnp.einsum('bsd,bse->de', xn, dq, preferred_element_type=F32)]
  transfers between devices with their start and end apart: 3 -> 5, of which waited for: 3 -> 5; matrix products, arithmetic and copies ran while one was open for 9% -> 4% of each run, Pallas kernels for 6% -> 12%
where the time goes in v2:
time: 1220 us; the launch traced here: 1210 us
  Pallas kernels  606 us (50%)
  waiting for transfers between devices  362 us (30%)
  matrix products  166 us (14%)
  other arithmetic  29.2 us (2%)
  blocking collectives  24 us (2%)
  between operations  14.1 us (1%)
    pallas_call x4, Pallas kernels, attend(): pl.pallas_call(functools.partial(attention_kernel, batch, first, last, sc...  439 us
    psum x3, waiting for transfers between devices, local_block(): d_wo, d_wq = lax.psum((d_wo, d_wq), 'sp', axis_index_groups=[order])  354 us
    pallas_call x1, Pallas kernels, local_block(): pl.pallas_call(post_kernel, grid=(batch // nb2,), in_specs=[rows_spec(nb2...  62.4 us
    dot_general x4, matrix products, local_block(): d_wo = jnp.einsum('bse,bsd->ed', o, dy, preferred_element_type=F32)  57.6 us
    dot_general x4, matrix products, local_block(): d_wq = jnp.einsum('bsd,bse->de', xn, dq, preferred_element_type=F32)  57.1 us
    pallas_call x1, Pallas kernels, local_block(): pl.pallas_call(out_kernel, grid=(batch // nb,), in_specs=[rows_spec(nb, c...  43.7 us
    pallas_call x1, Pallas kernels, local_block(): pl.pallas_call(functools.partial(query_kernel, scale=scale), grid=(batch...  43.2 us
    dot_general x1, matrix products, local_block(): jnp.einsum('bsd,ed->bse', dy, w_o, preferred_element_type=F32).astype(BF16)  41.8 us
  transfers between devices with their start and end apart: 5, of which 5 were waited for; matrix products, arithmetic and copies ran while one was open for 4% of the time, Pallas kernels for 12%

profile of v2, /device:TPU:0, one launch (start us, length us, event | category | flops | bytes accessed | tf_op | source)
XLA Modules:
  0.0 1211.8 jit_solution(4494834126651044029)
XLA Ops:
  12.2 17.0 %norm.1 = (bf16[32,128,2048]{2,1,0:T(8,128)(2,1)}, bf16[32,128,256]{2,1,0:T(8,128)(2,1)}) custom-call(bf16[32,128,2048]{2,1,0:T(8,128)(2,1)} %refs_7_, f32[1,2048]{1,0:T(1,128)} %bitcast.45, bf16[2048,256]{1,0:T(8,128)(2,1)} %copy-done.6, f32[128,128]{1,0:T(8,128)} %get-tuple-element.91.cos_ref.refs_6_, f32[128,128]{1,0:T(8,128)} %get-tuple-element.92.sin_ref.refs_7_), custom_call_target="tpu_custom_call" | custom-call | flops 4294967296 | bytes 33554432 | tf_op jit(solution)/shard_map/norm/pallas_call | solution.py:336
  29.2 43.2 %query.1.refs_1_.refs_3_ = bf16[32,128,2048]{2,1,0:T(8,128)(2,1)} custom-call(bf16[32,128,2048]{2,1,0:T(8,128)(2,1)} %get-tuple-element.40.xn_ref, bf16[2048,2048]{1,0:T(8,128)(2,1)} %refs_5_.2, f32[128,128]{1,0:T(8,128)} %get-tuple-element.91.cos_ref.refs_6_, f32[128,128]{1,0:T(8,128)} %get-tuple-element.92.sin_ref.refs_7_), custom_call_target="tpu_custom_call" | custom-call | flops 34359738368 | bytes 33554432 | tf_op jit(solution)/shard_map/query/pallas_call | solution.py:349
  72.4 41.8 %convolution_convert_fusion.refs_2_.refs_4_ = bf16[32,128,2048]{2,1,0:T(8,128)(2,1)} fusion(bf16[32,128,2048]{2,1,0:T(8,128)(2,1)} %refs_8_, bf16[2048,2048]{1,0:T(8,128)(2,1)} %refs_4_.1), kind=kOutput, calls=%fused_computation.2 | convolution fusion | flops 34368126976 | bytes 41943040 | tf_op jit(solution)/shard_map/bsd,ed->bse/dot_general | solution.py:360
  117.0 74.3 %attend.4 = (bf16[32,128,512]{2,1,0:T(8,128)(2,1)}, bf16[32,128,512]{2,1,0:T(8,128)(2,1)}, f32[32,2,4,2,128,128]{5,4,3,2,1,0:T(8,128)}) custom-call(s32[32,8,128]{2,1,0:T(8,128)} %broadcast_in_dim.2.refs_0_, bf16[32,128,2048]{2,1,0:T(8,128)(2,1)} %query.1.refs_1_.refs_3_, bf16[32,128,2048]{2,1,0:T(8,128)(2,1)} %convolution_convert_fusion.refs_2_.refs_4_, ...), custom_call_target="tpu_custom_call" | custom-call | flops 25769803776 | bytes 25165824 | tf_op jit(solution)/shard_map/attend/pallas_call | solution.py:401
  191.4 15.3 %convolution_bitcast_fusion.7 = f32[512,2048]{1,0:T(8,128)} fusion(bf16[32,128,512]{2,1,0:T(8,128)(2,1)} %get-tuple-element.42.refs_0_, bf16[32,128,2048]{2,1,0:T(8,128)(2,1)} %refs_8_), kind=kOutput, calls=%fused_computation.11 | convolution fusion | flops 8589934592 | bytes 25165824 | tf_op jit(solution)/shard_map/bse,bsd->ed/dot_general | solution.py:421
  206.6 13.9 %convolution_bitcast_fusion.6 = f32[2048,512]{1,0:T(8,128)} fusion(bf16[32,128,2048]{2,1,0:T(8,128)(2,1)} %get-tuple-element.40.xn_ref, bf16[32,128,512]{2,1,0:T(8,128)(2,1)S(1)} %copy-done.10), kind=kOutput, calls=%fused_computation.10 | convolution fusion | flops 8589934592 | bytes 25165824 | tf_op jit(solution)/shard_map/bsd,bse->de/dot_general | solution.py:422
  220.5 76.1 %attend.5 = (bf16[32,128,512]{2,1,0:T(8,128)(2,1)}, bf16[32,128,512]{2,1,0:T(8,128)(2,1)}, f32[32,2,4,2,128,128]{5,4,3,2,1,0:T(8,128)}) custom-call(s32[32,8,128]{2,1,0:T(8,128)} %broadcast_in_dim.2.refs_0_, bf16[32,128,2048]{2,1,0:T(8,128)(2,1)} %query.1.refs_1_.refs_3_, bf16[32,128,2048]{2,1,0:T(8,128)(2,1)} %convolution_convert_fusion.refs_2_.refs_4_, ...), custom_call_target="tpu_custom_call" | custom-call | flops 25769803776 | bytes 25165824 | tf_op jit(solution)/shard_map/attend/pallas_call | solution.py:401
  296.6 15.1 %convolution_bitcast_fusion.5 = f32[512,2048]{1,0:T(8,128)} fusion(bf16[32,128,512]{2,1,0:T(8,128)(2,1)} %get-tuple-element.47.refs_1_, bf16[32,128,2048]{2,1,0:T(8,128)(2,1)} %refs_8_), kind=kOutput, calls=%fused_computation.9 | convolution fusion | flops 8589934592 | bytes 25165824 | tf_op jit(solution)/shard_map/bse,bsd->ed/dot_general | solution.py:421
  311.8 14.1 %convolution_bitcast_fusion.4 = f32[2048,512]{1,0:T(8,128)} fusion(bf16[32,128,2048]{2,1,0:T(8,128)(2,1)} %get-tuple-element.40.xn_ref, bf16[32,128,512]{2,1,0:T(8,128)(2,1)S(1)} %copy-done.8), kind=kOutput, calls=%fused_computation.8 | convolution fusion | flops 8589934592 | bytes 25165824 | tf_op jit(solution)/shard_map/bsd,bse->de/dot_general | solution.py:422
  325.8 76.2 %attend.6 = (bf16[32,128,512]{2,1,0:T(8,128)(2,1)}, bf16[32,128,512]{2,1,0:T(8,128)(2,1)}, f32[32,2,4,2,128,128]{5,4,3,2,1,0:T(8,128)}) custom-call(s32[32,8,128]{2,1,0:T(8,128)} %broadcast_in_dim.2.refs_0_, bf16[32,128,2048]{2,1,0:T(8,128)(2,1)} %query.1.refs_1_.refs_3_, bf16[32,128,2048]{2,1,0:T(8,128)(2,1)} %convolution_convert_fusion.refs_2_.refs_4_, ...), custom_call_target="tpu_custom_call" | custom-call | flops 25769803776 | bytes 25165824 | tf_op jit(solution)/shard_map/attend/pallas_call | solution.py:401
  402.0 15.1 %convolution_bitcast_fusion.3 = f32[512,2048]{1,0:T(8,128)} fusion(bf16[32,128,512]{2,1,0:T(8,128)(2,1)} %get-tuple-element.52.refs_2_, bf16[32,128,2048]{2,1,0:T(8,128)(2,1)} %refs_8_), kind=kOutput, calls=%fused_computation.7 | convolution fusion | flops 8589934592 | bytes 25165824 | tf_op jit(solution)/shard_map/bse,bsd->ed/dot_general | solution.py:421
  417.1 13.8 %convolution_bitcast_fusion.2 = f32[2048,512]{1,0:T(8,128)} fusion(bf16[32,128,2048]{2,1,0:T(8,128)(2,1)} %get-tuple-element.40.xn_ref, bf16[32,128,512]{2,1,0:T(8,128)(2,1)S(1)} %copy-done.9), kind=kOutput, calls=%fused_computation.6 | convolution fusion | flops 8589934592 | bytes 25165824 | tf_op jit(solution)/shard_map/bsd,bse->de/dot_general | solution.py:422
  431.0 212.7 %attend.7 = (bf16[32,128,512]{2,1,0:T(8,128)(2,1)}, bf16[32,128,512]{2,1,0:T(8,128)(2,1)}, f32[32,128,256]{2,1,0:T(8,128)}) custom-call(s32[32,8,128]{2,1,0:T(8,128)} %broadcast_in_dim.2.refs_0_, bf16[32,128,2048]{2,1,0:T(8,128)(2,1)} %query.1.refs_1_.refs_3_, bf16[32,128,2048]{2,1,0:T(8,128)(2,1)} %convolution_convert_fusion.refs_2_.refs_4_, ...), custom_call_target="tpu_custom_call" | custom-call | flops 25769803776 | bytes 25165824 | tf_op jit(solution)/shard_map/attend/pallas_call | solution.py:401
  647.4 15.4 %convolution_bitcast_fusion = f32[2048,512]{1,0:T(8,128)} fusion(bf16[32,128,2048]{2,1,0:T(8,128)(2,1)} %get-tuple-element.40.xn_ref, bf16[32,128,512]{2,1,0:T(8,128)(2,1)} %get-tuple-element.58.refs_3_), kind=kOutput, calls=%fused_computation.4 | convolution fusion | flops 8589934592 | bytes 25165824 | tf_op jit(solution)/shard_map/bsd,bse->de/dot_general | solution.py:422
  662.9 12.0 convolution_bitcast_fusion.1
  675.7 9.9 convolution_bitcast_fusion.8
  688.6 62.4 %norm_grad.1 = (bf16[32,128,2048]{2,1,0:T(8,128)(2,1)}, f32[8,2048]{1,0:T(8,128)}) custom-call(bf16[32,128,512]{2,1,0:T(8,128)(2,1)} %get-tuple-element.43.refs_0_, bf16[32,128,512]{2,1,0:T(8,128)(2,1)} %get-tuple-element.48.refs_1_, bf16[32,128,512]{2,1,0:T(8,128)(2,1)} %get-tuple-element.53.refs_2_, bf16[32,128,512]{2,1,0:T(8,128)(2,1)} %get-tuple-element.58.refs_3_, ...), custom_call_target="tpu_custom_call" | custom-call | flops 38654705664 | bytes 67108864 | tf_op jit(solution)/shard_map/norm_grad/pallas_call | solution.py:442
  751.8 24.0 %psum.79 = f32[2048]{0:T(1024)} all-reduce(f32[2048]{0:T(1024)S(1)} %reduce_sum.9), channel_id=1, replica_groups=mesh['sp'=8] {'sp'}, use_global_device_ids=true, to_apply=%region_10.0 | all-reduce | flops 2048 | bytes 16384 | tf_op jit(solution)/shard_map/psum | solution.py:455
  775.8 43.7 %output.1 = bf16[32,128,2048]{2,1,0:T(8,128)(2,1)} custom-call(bf16[32,128,512]{2,1,0:T(8,128)(2,1)} %get-tuple-element.42.refs_0_, bf16[32,128,512]{2,1,0:T(8,128)(2,1)} %get-tuple-element.47.refs_1_, bf16[32,128,512]{2,1,0:T(8,128)(2,1)} %get-tuple-element.52.refs_2_, bf16[32,128,512]{2,1,0:T(8,128)(2,1)} %get-tuple-element.57.refs_3_, ...), custom_call_target="tpu_custom_call" | custom-call | flops 34359738368 | bytes 50331648 | tf_op jit(solution)/shard_map/output/pallas_call | solution.py:456
  827.7 115.9 %all-reduce.11.cloned.1.call-done = (f32[2048,512]{1,0:T(8,128)}, f32[512,2048]{1,0:T(8,128)}) async-done(((f32[2048,512]{1,0:T(8,128)}, f32[512,2048]{1,0:T(8,128)}), (f32[2048,512]{1,0:T(8,128)}, f32[512,2048]{1,0:T(8,128)})) %all-reduce.11.cloned.1.call-update) | async-done | bytes 8388624 | tf_op jit(solution)/shard_map/psum | solution.py:426
  943.6 118.8 %all-reduce.13.cloned.1.call-done = (f32[2048,512]{1,0:T(8,128)}, f32[512,2048]{1,0:T(8,128)}) async-done(((f32[2048,512]{1,0:T(8,128)}, f32[512,2048]{1,0:T(8,128)}), (f32[2048,512]{1,0:T(8,128)}, f32[512,2048]{1,0:T(8,128)})) %all-reduce.13.cloned.1.call-update) | async-done | bytes 8388624 | tf_op jit(solution)/shard_map/psum | solution.py:426
  1062.4 118.8 %all-reduce.15.cloned.1.call-done = (f32[2048,512]{1,0:T(8,128)}, f32[512,2048]{1,0:T(8,128)}) async-done(((f32[2048,512]{1,0:T(8,128)}, f32[512,2048]{1,0:T(8,128)}), (f32[2048,512]{1,0:T(8,128)}, f32[512,2048]{1,0:T(8,128)})) %all-reduce.15.cloned.1.call-update) | async-done | bytes 8388624 | tf_op jit(solution)/shard_map/psum | solution.py:426
  1181.2 13.4 %pad_maximum_fusion = f32[2048,2048]{1,0:T(8,128)} fusion(f32[2048,512]{1,0:T(8,128)} %get-tuple-element.73, f32[2048,512]{1,0:T(8,128)} %get-tuple-element.80, f32[2048,512]{1,0:T(8,128)} %get-tuple-element.78, f32[2048,512]{1,0:T(8,128)} %get-tuple-element.76), kind=kLoop, calls=%fused_computation | loop fusion | flops 12582912 | bytes 33554432 | tf_op jit(solution)/shard_map/concatenate | solution.py:439
  1197.8 7.3 pad_maximum_fusion.1
  (58 shorter events, 27.5 us)
Async XLA Ops:
  7.2 109.1 %all-gather.3.cloned.1.call-start = ((), (), s32[]{:S(2)}) async-start(), calls=%async_computation | async-start | bytes 18874368 | tf_op jit(solution)/shard_map/all_gather | solution.py:348
  11.2 1.0 copy-start.6
  29.2 795.5 %all-reduce.9.cloned.1.call-start = ((), (), s32[]{:S(2)}) async-start(), calls=%async_computation.1 | async-start | bytes 20971520 | tf_op jit(solution)/shard_map/psum | solution.py:435
  72.4 43.9 %copy-start.7 = (s32[32]{0:T(128)S(1)}, s32[32]{0:T(128)}, u32[]{:S(2)}) copy-start(s32[32]{0:T(128)} %param.10) | copy-start | bytes 388
  191.4 15.3 %copy-start.10 = (bf16[32,128,512]{2,1,0:T(8,128)(2,1)S(1)}, bf16[32,128,512]{2,1,0:T(8,128)(2,1)}, u32[]{:S(2)}) copy-start(bf16[32,128,512]{2,1,0:T(8,128)(2,1)} %get-tuple-element.43.refs_0_) | copy-start | bytes 12582916
  296.6 15.1 %copy-start.8 = (bf16[32,128,512]{2,1,0:T(8,128)(2,1)S(1)}, bf16[32,128,512]{2,1,0:T(8,128)(2,1)}, u32[]{:S(2)}) copy-start(bf16[32,128,512]{2,1,0:T(8,128)(2,1)} %get-tuple-element.48.refs_1_) | copy-start | bytes 12582916
  402.0 15.1 %copy-start.9 = (bf16[32,128,512]{2,1,0:T(8,128)(2,1)S(1)}, bf16[32,128,512]{2,1,0:T(8,128)(2,1)}, u32[]{:S(2)}) copy-start(bf16[32,128,512]{2,1,0:T(8,128)(2,1)} %get-tuple-element.53.refs_2_) | copy-start | bytes 12582916
  646.6 16.2 %slice-start = ((s8[16777216]{0:T(1024)(128)(4,1)}), s8[4194304]{0:T(1024)(128)(4,1)S(1)}, s32[]{:S(2)}) async-start(s8[16777216]{0:T(1024)(128)(4,1)} %bitcast.47), calls=%async_computation.5 | async-start | bytes 8388608
  647.4 15.4 %slice-start.1 = ((s8[16777216]{0:T(1024)(128)(4,1)}), s8[4194304]{0:T(1024)(128)(4,1)S(1)}, s32[]{:S(2)}) async-start(s8[16777216]{0:T(1024)(128)(4,1)} %bitcast.47), calls=%async_computation.6 | async-start | bytes 8388608
  647.4 15.4 %slice-start.2 = ((s8[16777216]{0:T(1024)(128)(4,1)}), s8[4194304]{0:T(1024)(128)(4,1)S(1)}, s32[]{:S(2)}) async-start(s8[16777216]{0:T(1024)(128)(4,1)} %bitcast.47), calls=%async_computation.7 | async-start | bytes 8388608
  647.4 15.4 %slice-start.3 = ((s8[16777216]{0:T(1024)(128)(4,1)}), s8[4194304]{0:T(1024)(128)(4,1)S(1)}, s32[]{:S(2)}) async-start(s8[16777216]{0:T(1024)(128)(4,1)} %bitcast.47), calls=%async_computation.8 | async-start | bytes 8388608
  662.8 12.1 copy-start.4
  662.9 12.1 copy-start.5
  685.6 258.0 %all-reduce.11.cloned.1.call-start = ((), (), s32[]{:S(2)}) async-start(), calls=%async_computation.2 | async-start | bytes 16777216 | tf_op jit(solution)/shard_map/psum | solution.py:426
  686.4 376.1 %all-reduce.13.cloned.1.call-start = ((), (), s32[]{:S(2)}) async-start(), calls=%async_computation.3 | async-start | bytes 16777216 | tf_op jit(solution)/shard_map/psum | solution.py:426
  686.9 494.3 %all-reduce.15.cloned.1.call-start = ((), (), s32[]{:S(2)}) async-start(), calls=%async_computation.4 | async-start | bytes 16777216 | tf_op jit(solution)/shard_map/psum | solution.py:426
  1181.2 13.4 %copy-start = (f32[512,2048]{1,0:T(8,128)S(1)}, f32[512,2048]{1,0:T(8,128)}, u32[]{:S(2)}) copy-start(f32[512,2048]{1,0:T(8,128)} %get-tuple-element.75) | copy-start | bytes 12582916
  1181.2 13.6 %copy-start.1 = (f32[512,2048]{1,0:T(8,128)S(1)}, f32[512,2048]{1,0:T(8,128)}, u32[]{:S(2)}) copy-start(f32[512,2048]{1,0:T(8,128)} %get-tuple-element.77) | copy-start | bytes 12582916
  1181.2 15.4 %copy-start.2 = (f32[512,2048]{1,0:T(8,128)S(1)}, f32[512,2048]{1,0:T(8,128)}, u32[]{:S(2)}) copy-start(f32[512,2048]{1,0:T(8,128)} %get-tuple-element.79) | copy-start | bytes 12582916
  1181.2 16.6 %copy-start.3 = (f32[512,2048]{1,0:T(8,128)S(1)}, f32[512,2048]{1,0:T(8,128)}, u32[]{:S(2)}) copy-start(f32[512,2048]{1,0:T(8,128)} %get-tuple-element.81) | copy-start | bytes 12582916
Sparse Core Ops, SparseCore 0:
  29.3 86.9 all-gather.2
  685.7 138.8 all-reduce.8
  828.4 115.1 all-reduce.10
  947.2 115.2 all-reduce.12
  1066.0 115.2 all-reduce.14

commit v3 on v2

--- a/solution.py
+++ b/solution.py
@@ -14,7 +14,10 @@
 F32 = jnp.float32
 BF16 = jnp.bfloat16
 MESH = pl.DeviceIdType.MESH
-CHUNKS = 4
+CHUNKS = 2
+SUBS = 2
+SLOTS = 3
+LAG = 3
 VMEM_LIMIT = 60 * 1024 * 1024
 NT = (((1,), (1,)), ((), ()))
 
@@ -73,6 +76,7 @@
         (part, recv1, sum1, recv2, sum2, recv3,
          send1, got1, send2, got2, send3, got3, free1, free2, free3) = refs[13:]
     t = pl.program_id(0)
+    steps = SUBS * batch
     me = lax.axis_index('sp')
     core = me % 2
     x_bit = (me // 2) % 2
@@ -127,7 +131,13 @@
 
     low = functools.partial(jnp.full, (8, 2 * hd), MASK_FILL, F32)
 
-    @pl.when(t <= batch)
+    acc = part.at[((t + SUBS - 1) // SUBS + SLOTS - 1) % SLOTS] if last else dkv_ref.at[0]
+
+    @pl.when((t % SUBS == 1 % SUBS) & (t <= steps))
+    def _():
+        acc[...] = jnp.zeros(acc.shape, F32) if first else carry_ref[0]
+
+    @pl.when(t <= steps)
     def _():
         now, was = t % 2, (t + 1) % 2
         k_all = kv_ref[:, 0, :, :hd].reshape(keys, hd)
@@ -138,8 +148,6 @@
         v_scr[now] = v_all
         k_t[now] = k_all.T
         v_t[now] = v_all.T
-        acc = part.at[was] if last else dkv_ref.at[0]
-        acc[...] = jnp.zeros(acc.shape, F32) if first else carry_ref[0]
 
         def score_step(i):
             buf = i
@@ -208,59 +216,72 @@
     if not last:
         return
 
-    @pl.when(t >= 4)
-    def _():
-        slot = t % 2
+    def stage(number):
+        ahead = t - LAG * number
+        b = ahead // SUBS - 1
+        return b, (ahead >= SUBS) & (ahead % SUBS == 0) & (b < batch)
+
+    b4, due4 = stage(3)
+
+    @pl.when(due4)
+    def _():
+        slot = b4 % SLOTS
         copy_3(slot).wait()
         done = sum2[slot, bit_2] + recv3[slot]
         dkv_ref[0, :, :hd] = done[0]
         dkv_ref[0, :, hd:] = done[1]
 
-        @pl.when(t - 4 < batch - 2)
+        @pl.when(b4 + SLOTS < batch)
         def _():
             pl.semaphore_signal(free3.at[slot], inc=1, device_id=(near_2,), device_id_type=MESH)
 
-    @pl.when((t >= 3) & (t - 3 < batch))
-    def _():
-        slot = (t + 1) % 2
+    b3, due3 = stage(2)
+
+    @pl.when(due3)
+    def _():
+        slot = b3 % SLOTS
         copy_2(slot).wait()
         for s in range(2):
             sum2[slot, s] = sum1[slot, bit_1, s] + recv2[slot, s]
 
-        @pl.when(t - 3 < batch - 2)
+        @pl.when(b3 + SLOTS < batch)
         def _():
             pl.semaphore_signal(free2.at[slot], inc=1, device_id=(near_1,), device_id_type=MESH)
 
-        @pl.when(t - 3 >= 2)
+        @pl.when(b3 >= SLOTS)
         def _():
             pl.semaphore_wait(free3.at[slot], 1)
 
         copy_3(slot).start()
 
-    @pl.when((t >= 2) & (t - 2 < batch))
-    def _():
-        slot = t % 2
+    b2, due2 = stage(1)
+
+    @pl.when(due2)
+    def _():
+        slot = b2 % SLOTS
         copy_1(slot).wait()
         for f in range(2):
             for s in range(2):
                 chip = f * (1 + core) + s * (2 - core)
                 sum1[slot, f, s] = part[slot, core, chip] + recv1[slot, chip]
 
-        @pl.when(t - 2 < batch - 2)
+        @pl.when(b2 + SLOTS < batch)
         def _():
             pl.semaphore_signal(free1.at[slot], inc=1, device_id=(partner,), device_id_type=MESH)
 
-        @pl.when(t - 2 >= 2)
+        @pl.when(b2 >= SLOTS)
         def _():
             pl.semaphore_wait(free2.at[slot], 1)
 
         copy_2(slot).start()
 
-    @pl.when((t >= 1) & (t - 1 < batch))
-    def _():
-        slot = (t + 1) % 2
-
-        @pl.when(t - 1 >= 2)
+    b1, due1 = stage(0)
+
+    @pl.when(due1)
+    def _():
+        slot = b1 % SLOTS
+
+        @pl.when(b1 >= SLOTS)
         def _():
             pl.semaphore_wait(free1.at[slot], 1)
 
@@ -359,7 +380,6 @@
         )(xn, w_q, cos2, sin2)
         d_o = jnp.einsum('bsd,ed->bse', dy, w_o, preferred_element_type=F32).astype(BF16)
 
-        end = batch - 1
         f32_tile = (seq, hd)
         prefix = jnp.broadcast_to(prefix_len[:, None, None], (batch, 8, hd))
         cols = width // CHUNKS
@@ -367,15 +387,17 @@
 
         def attend(n, q, d_o, carry):
             first, last = n == 0, n == CHUNKS - 1
-            before = lambda i: jnp.clip(i - 1, 0, end)
-            here = lambda i: (before(i), 0, 0)
-            part_spec = pl.BlockSpec((1,) + split, lambda i: (before(i), 0, 0, 0, 0, 0))
-            in_specs = [pl.BlockSpec((1, 8, hd), lambda i: (jnp.minimum(i, end), 0, 0)),
-                        pl.BlockSpec((1, seq, cols), lambda i: (jnp.minimum(i, end), 0, n)),
-                        pl.BlockSpec((1, seq, cols), lambda i: (jnp.minimum(i, end), 0, n)),
-                        pl.BlockSpec((1, seq, cols), lambda i: (before(i), 0, n)),
-                        pl.BlockSpec((1, seq, cols), lambda i: (before(i), 0, n)),
-                        pl.BlockSpec((groups, 1, seq, 2 * hd), lambda i: (0, jnp.minimum(i, end), 0, 0)),
+            top = SUBS * batch - 1
+            now = lambda i: jnp.minimum(i, top)
+            before = lambda i: jnp.clip(i - 1, 0, top)
+            wide = cols // SUBS
+            here = lambda i: (before(i) // SUBS, 0, before(i) % SUBS)
+            part_spec = pl.BlockSpec((1,) + split, lambda i: (before(i) // SUBS, 0, 0, 0, 0, 0))
+            at_now = pl.BlockSpec((1, seq, wide), lambda i: (now(i) // SUBS, 0, SUBS * n + now(i) % SUBS))
+            at_before = pl.BlockSpec((1, seq, wide), lambda i: (before(i) // SUBS, 0, SUBS * n + before(i) % SUBS))
+            in_specs = [pl.BlockSpec((1, 8, hd), lambda i: (now(i) // SUBS, 0, 0)),
+                        at_now, at_now, at_before, at_before,
+                        pl.BlockSpec((groups, 1, seq, 2 * hd), lambda i: (0, now(i) // SUBS, 0, 0)),
                         full(seq, hd), full(seq, hd)]
             args = [prefix, q, d_o, q, d_o, kv_all, cos2, sin2]
             if not first:
@@ -388,21 +410,20 @@
                 pltpu.VMEM((seq, seq), BF16), pltpu.VMEM((2, 8, 2 * hd), F32), pltpu.VMEM((2, 8, 2 * hd), F32)]
             params = dict(vmem_limit_bytes=VMEM_LIMIT)
             if last:
-                dkv_spec = pl.BlockSpec((1, seq, 2 * hd), lambda i: (jnp.maximum(i - 4, 0), 0, 0))
+                dkv_spec = pl.BlockSpec((1, seq, 2 * hd), lambda i: (jnp.maximum(i - SUBS - 3 * LAG, 0) // SUBS, 0, 0))
                 dkv_shape = jax.ShapeDtypeStruct((batch, seq, 2 * hd), F32)
-                scratch += [pltpu.VMEM((2,) + split, F32), pltpu.VMEM((2, 4, 2) + f32_tile, F32),
-                            pltpu.VMEM((2, 2, 2, 2) + f32_tile, F32), pltpu.VMEM((2, 2, 2) + f32_tile, F32),
-                            pltpu.VMEM((2, 2, 2) + f32_tile, F32), pltpu.VMEM((2, 2) + f32_tile, F32)]
-                scratch += [pltpu.SemaphoreType.DMA((2,))] * 6 + [pltpu.SemaphoreType.REGULAR((2,))] * 3
+                scratch += [pltpu.VMEM((SLOTS,) + shape + f32_tile, F32) for shape in
+                            ((2, groups // 2, 2), (4, 2), (2, 2, 2), (2, 2), (2, 2), (2,))]
+                scratch += [pltpu.SemaphoreType.DMA((SLOTS,))] * 6 + [pltpu.SemaphoreType.REGULAR((SLOTS,))] * 3
                 params.update(collective_id=0, has_side_effects=True)
             else:
                 dkv_spec = part_spec
                 dkv_shape = jax.ShapeDtypeStruct((batch,) + split, F32)
             return pl.pallas_call(
                 functools.partial(attention_kernel, batch, first, last, scale=scale),
-                grid=(batch + 1 + 3 * last,),
+                grid=(SUBS * batch + 1 + 3 * LAG * last,),
                 in_specs=in_specs,
-                out_specs=[pl.BlockSpec((1, seq, cols), here), pl.BlockSpec((1, seq, cols), here), dkv_spec],
+                out_specs=[pl.BlockSpec((1, seq, wide), here), pl.BlockSpec((1, seq, wide), here), dkv_spec],
                 out_shape=[jax.ShapeDtypeStruct((batch, seq, cols), BF16),
                            jax.ShapeDtypeStruct((batch, seq, cols), BF16), dkv_shape],
                 scratch_shapes=scratch,
@@ -419,20 +440,22 @@
             os.append(o)
             dqs.append(dq)
             d_wo = jnp.einsum('bse,bsd->ed', o, dy, preferred_element_type=F32)
-            d_wq = jnp.einsum('bsd,bse->de', xn, dq, preferred_element_type=F32)
             if n < CHUNKS - 1:
+                d_wq = jnp.einsum('bsd,bse->de', xn, dq, preferred_element_type=F32)
                 d_wo, d_wq, q, carry = lax.optimization_barrier((d_wo, d_wq, q, carry))
-                order = [m ^ (n + 1) for m in range(groups)]
-                d_wo, d_wq = lax.psum((d_wo, d_wq), 'sp', axis_index_groups=[order])
+                d_wo, d_wq = lax.psum((d_wo, d_wq), 'sp', axis_index_groups=[[m ^ 1 for m in range(groups)]])
             else:
+                d_wo, xn = lax.optimization_barrier((d_wo, xn))
+                d_wo = lax.psum(d_wo, 'sp', axis_index_groups=[[m ^ 2 for m in range(groups)]])
+                d_wq = jnp.einsum('bsd,bse->de', xn, dq, preferred_element_type=F32)
                 dkv = carry
                 rot = dkv[..., :hd].astype(BF16).astype(F32)
                 rolled = jnp.concatenate([rot[..., half:], rot[..., :half]], axis=-1)
                 dk_proj = (rot * cos2 - rolled * sin2).astype(BF16)
                 dkv_proj = jnp.concatenate([dk_proj, dkv[..., hd:].astype(BF16)], axis=-1)
                 d_wkv = jnp.einsum('bsd,bse->de', xn, dkv_proj, preferred_element_type=F32)
-                d_wo, d_wq, d_wkv, x_b, dy_b = lax.optimization_barrier((d_wo, d_wq, d_wkv, x, dy))
-                d_wo, d_wq, d_wkv = lax.psum((d_wo, d_wq, d_wkv), 'sp')
+                d_wq, d_wkv, x_b, dy_b = lax.optimization_barrier((d_wq, d_wkv, x, dy))
+                d_wq, d_wkv = lax.psum((d_wq, d_wkv), 'sp')
             d_wos.append(d_wo)
             d_wqs.append(d_wq)
         d_wo = jnp.concatenate(d_wos, axis=0)

time: 1220 us -> 1060 us (0.87)
  Pallas kernels: 606 us -> 502 us
  waiting for transfers between devices: 362 us -> 322 us
  matrix products: 166 us -> 142 us
    pallas_call x4 -> x2, Pallas kernels: 439 us -> 336 us  [attend(): pl.pallas_call(functools.partial(attention_kernel, batch, first, last, sc...]
    psum x4 -> x3, waiting for transfers between devices: 359 us -> 320 us  [the longest x1 208 us: local_block(): lax.psum((d_wo, d_wq), 'sp', axis_index_groups=[[m ^ 1 for m in range(gro...]
    dot_general x4 -> x2, matrix products: 57.1 us -> 46.2 us  [local_block(): d_wq = jnp.einsum('bsd,bse->de', xn, dq, preferred_element_type=F32)]
    dot_general x4 -> x2, matrix products: 57.6 us -> 46.9 us  [local_block(): d_wo = jnp.einsum('bse,bsd->ed', o, dy, preferred_element_type=F32)]
  transfers between devices with their start and end apart: 5 -> 4, of which waited for: 5 -> 4; matrix products, arithmetic and copies ran while one was open for 4% -> 6% of each run, Pallas kernels for 12% -> 14%
where the time goes in v3:
time: 1060 us; the launch traced here: 1050 us
  Pallas kernels  502 us (47%)
  waiting for transfers between devices  322 us (30%)
  matrix products  142 us (13%)
  other arithmetic  34.9 us (3%)
  blocking collectives  24.1 us (2%)
  between operations  14.2 us (1%)
    pallas_call x2, Pallas kernels, attend(): pl.pallas_call(functools.partial(attention_kernel, batch, first, last, sc...  336 us
    psum x1, waiting for transfers between devices, local_block(): lax.psum((d_wo, d_wq), 'sp', axis_index_groups=[[m ^ 1 for m in range(gro...  208 us
    psum x1, waiting for transfers between devices, local_block(): lax.psum(d_wo, 'sp', axis_index_groups=[[m ^ 2 for m in range(groups)]])  106 us
    pallas_call x1, Pallas kernels, local_block(): pl.pallas_call(post_kernel, grid=(batch // nb2,), in_specs=[rows_spec(nb2...  62.2 us
    dot_general x2, matrix products, local_block(): d_wo = jnp.einsum('bse,bsd->ed', o, dy, preferred_element_type=F32)  46.9 us
    dot_general x2, matrix products, local_block(): d_wq = jnp.einsum('bsd,bse->de', xn, dq, preferred_element_type=F32)  46.2 us
    pallas_call x1, Pallas kernels, local_block(): pl.pallas_call(out_kernel, grid=(batch // nb,), in_specs=[rows_spec(nb, c...  43.8 us
    pallas_call x1, Pallas kernels, local_block(): pl.pallas_call(functools.partial(query_kernel, scale=scale), grid=(batch...  43.2 us
  transfers between devices with their start and end apart: 4, of which 4 were waited for; matrix products, arithmetic and copies ran while one was open for 6% of the time, Pallas kernels for 14%

profile of v3, /device:TPU:0, one launch (start us, length us, event | category | flops | bytes accessed | tf_op | source)
XLA Modules:
  0.0 1048.7 jit_solution(14957634399959815677)
XLA Ops:
  12.2 17.0 %norm.1 = (bf16[32,128,2048]{2,1,0:T(8,128)(2,1)}, bf16[32,128,256]{2,1,0:T(8,128)(2,1)}) custom-call(bf16[32,128,2048]{2,1,0:T(8,128)(2,1)} %refs_5_, f32[1,2048]{1,0:T(1,128)} %bitcast.25, bf16[2048,256]{1,0:T(8,128)(2,1)} %copy-done.2, f32[128,128]{1,0:T(8,128)} %get-tuple-element.60.cos_ref.refs_6_, f32[128,128]{1,0:T(8,128)} %get-tuple-element.61.sin_ref.refs_7_), custom_call_target="tpu_custom_call" | custom-call | flops 4294967296 | bytes 33554432 | tf_op jit(solution)/shard_map/norm/pallas_call | solution.py:357
  29.2 43.2 %query.1.refs_1_.refs_3_ = bf16[32,128,2048]{2,1,0:T(8,128)(2,1)} custom-call(bf16[32,128,2048]{2,1,0:T(8,128)(2,1)} %get-tuple-element.35.xn_ref, bf16[2048,2048]{1,0:T(8,128)(2,1)} %refs_3_.2, f32[128,128]{1,0:T(8,128)} %get-tuple-element.60.cos_ref.refs_6_, f32[128,128]{1,0:T(8,128)} %get-tuple-element.61.sin_ref.refs_7_), custom_call_target="tpu_custom_call" | custom-call | flops 34359738368 | bytes 33554432 | tf_op jit(solution)/shard_map/query/pallas_call | solution.py:370
  72.4 41.8 %convolution_convert_fusion.refs_2_.refs_4_ = bf16[32,128,2048]{2,1,0:T(8,128)(2,1)} fusion(bf16[32,128,2048]{2,1,0:T(8,128)(2,1)} %refs_6_, bf16[2048,2048]{1,0:T(8,128)(2,1)} %refs_2_.1), kind=kOutput, calls=%fused_computation.2 | convolution fusion | flops 34368126976 | bytes 41943040 | tf_op jit(solution)/shard_map/bsd,ed->bse/dot_general | solution.py:381
  114.2 2.1 all-gather.3.cloned.1.call-done
  117.1 152.0 %attend.2 = (bf16[32,128,1024]{2,1,0:T(8,128)(2,1)}, bf16[32,128,1024]{2,1,0:T(8,128)(2,1)}, f32[32,2,4,2,128,128]{5,4,3,2,1,0:T(8,128)}) custom-call(s32[32,8,128]{2,1,0:T(8,128)} %broadcast_in_dim.2.refs_0_, bf16[32,128,2048]{2,1,0:T(8,128)(2,1)} %query.1.refs_1_.refs_3_, bf16[32,128,2048]{2,1,0:T(8,128)(2,1)} %convolution_convert_fusion.refs_2_.refs_4_, ...), custom_call_target="tpu_custom_call" | custom-call | flops 51539607552 | bytes 50331648 | tf_op jit(solution)/shard_map/attend/pallas_call | solution.py:422
  269.1 25.0 %convolution_bitcast_fusion.3 = f32[1024,2048]{1,0:T(8,128)} fusion(bf16[32,128,1024]{2,1,0:T(8,128)(2,1)} %get-tuple-element.29.refs_0_, bf16[32,128,2048]{2,1,0:T(8,128)(2,1)} %refs_6_), kind=kOutput, calls=%fused_computation.7 | convolution fusion | flops 17179869184 | bytes 33554432 | tf_op jit(solution)/shard_map/bse,bsd->ed/dot_general | solution.py:442
  294.0 21.6 %convolution_bitcast_fusion.2 = f32[2048,1024]{1,0:T(8,128)} fusion(bf16[32,128,2048]{2,1,0:T(8,128)(2,1)} %get-tuple-element.35.xn_ref, bf16[32,128,1024]{2,1,0:T(8,128)(2,1)S(1)} %copy-done.6), kind=kOutput, calls=%fused_computation.6 | convolution fusion | flops 17179869184 | bytes 33554432 | tf_op jit(solution)/shard_map/bsd,bse->de/dot_general | solution.py:444
  315.7 183.8 %attend.3 = (bf16[32,128,1024]{2,1,0:T(8,128)(2,1)}, bf16[32,128,1024]{2,1,0:T(8,128)(2,1)}, f32[32,128,256]{2,1,0:T(8,128)}) custom-call(s32[32,8,128]{2,1,0:T(8,128)} %broadcast_in_dim.2.refs_0_, bf16[32,128,2048]{2,1,0:T(8,128)(2,1)} %query.1.refs_1_.refs_3_, bf16[32,128,2048]{2,1,0:T(8,128)(2,1)} %convolution_convert_fusion.refs_2_.refs_4_, ...), custom_call_target="tpu_custom_call" | custom-call | flops 51539607552 | bytes 50331648 | tf_op jit(solution)/shard_map/attend/pallas_call | solution.py:422
  499.4 2.6 convert.5
  502.5 2.7 fusion.5
  505.3 21.9 %convolution_bitcast_fusion.1 = f32[1024,2048]{1,0:T(8,128)} fusion(bf16[32,128,1024]{2,1,0:T(8,128)(2,1)S(1)} %bitcast.32, bf16[32,128,2048]{2,1,0:T(8,128)(2,1)} %refs_6_), kind=kOutput, calls=%fused_computation.5 | convolution fusion | flops 17179869184 | bytes 33554432 | tf_op jit(solution)/shard_map/bse,bsd->ed/dot_general | solution.py:442
  527.2 3.1 fusion.2
  530.3 24.6 %convolution_bitcast_fusion = f32[2048,1024]{1,0:T(8,128)} fusion(bf16[32,128,2048]{2,1,0:T(8,128)(2,1)} %get-tuple-element.35.xn_ref, bf16[32,128,1024]{2,1,0:T(8,128)(2,1)} %get-tuple-element.36.refs_1_), kind=kOutput, calls=%fused_computation.4 | convolution fusion | flops 17179869184 | bytes 33554432 | tf_op jit(solution)/shard_map/bsd,bse->de/dot_general | solution.py:450
  555.0 6.6 convolution_bitcast_fusion.4
  562.9 1.6 pad_maximum_fusion.2.refs_2_
  564.4 62.2 %norm_grad.1 = (bf16[32,128,2048]{2,1,0:T(8,128)(2,1)}, f32[8,2048]{1,0:T(8,128)}) custom-call(bf16[32,128,1024]{2,1,0:T(8,128)(2,1)} %get-tuple-element.30.refs_0_, bf16[32,128,1024]{2,1,0:T(8,128)(2,1)} %get-tuple-element.36.refs_1_, bf16[32,128,256]{2,1,0:T(8,128)(2,1)} %pad_maximum_fusion.2.refs_2_, bf16[2048,2048]{1,0:T(8,128)(2,1)} %refs_3_.2, ...), custom_call_target="tpu_custom_call" | custom-call | flops 38654705664 | bytes 67108864 | tf_op jit(solution)/shard_map/norm_grad/pallas_call | solution.py:465
  627.6 24.1 %psum.47 = f32[2048]{0:T(1024)} all-reduce(f32[2048]{0:T(1024)S(1)} %reduce_sum.9), channel_id=1, replica_groups=mesh['sp'=8] {'sp'}, use_global_device_ids=true, to_apply=%region_6.0 | all-reduce | flops 2048 | bytes 16384 | tf_op jit(solution)/shard_map/psum | solution.py:478
  651.7 43.8 %output.1 = bf16[32,128,2048]{2,1,0:T(8,128)(2,1)} custom-call(bf16[32,128,1024]{2,1,0:T(8,128)(2,1)} %get-tuple-element.29.refs_0_, bf16[32,128,1024]{2,1,0:T(8,128)(2,1)} %get-tuple-element.34.refs_1_, bf16[2048,2048]{1,0:T(8,128)(2,1)} %refs_2_.1, bf16[32,128,2048]{2,1,0:T(8,128)(2,1)} %refs_5_), custom_call_target="tpu_custom_call" | custom-call | flops 34359738368 | bytes 50331648 | tf_op jit(solution)/shard_map/output/pallas_call | solution.py:479
  695.4 5.4 all-reduce.8.cloned.1.call-done
  700.8 3.0 fusion.4
  703.8 207.8 %all-reduce.10.cloned.1.call-done = (f32[2048,1024]{1,0:T(8,128)}, f32[1024,2048]{1,0:T(8,128)}) async-done(((f32[2048,1024]{1,0:T(8,128)}, f32[1024,2048]{1,0:T(8,128)}), (f32[2048,1024]{1,0:T(8,128)}, f32[1024,2048]{1,0:T(8,128)})) %all-reduce.10.cloned.1.call-update) | async-done | bytes 16777232 | tf_op jit(solution)/shard_map/psum | solution.py:446
  911.6 12.0 %pad_maximum_fusion = f32[2048,2048]{1,0:T(8,128)} fusion(f32[2048,1024]{1,0:T(8,128)} %get-tuple-element.47, f32[2048,1024]{1,0:T(8,128)} %get-tuple-element.49), kind=kLoop, calls=%fused_computation | loop fusion | flops 4194304 | bytes 33554432 | tf_op jit(solution)/shard_map/concatenate | solution.py:462
  923.6 106.4 %all-reduce.6.cloned.1.call-done = f32[1024,2048]{1,0:T(8,128)} async-done(((f32[1024,2048]{1,0:T(8,128)}), f32[1024,2048]{1,0:T(8,128)}) %all-reduce.6.cloned.1.call-update) | async-done | bytes 8388624 | tf_op jit(solution)/shard_map/psum | solution.py:449
  1030.1 11.8 %pad_maximum_fusion.1 = f32[2048,2048]{1,0:T(8,128)} fusion(f32[1024,2048]{1,0:T(8,128)} %all-reduce.6.cloned.1.call-done, f32[1024,2048]{1,0:T(8,128)} %get-tuple-element.50), kind=kLoop, calls=%fused_computation.1 | loop fusion | flops 4194304 | bytes 33554432 | tf_op jit(solution)/shard_map/concatenate | solution.py:461
  (46 shorter events, 8.3 us)
Async XLA Ops:
  7.2 109.1 %all-gather.3.cloned.1.call-start = ((), (), s32[]{:S(2)}) async-start(), calls=%async_computation.1 | async-start | bytes 18874368 | tf_op jit(solution)/shard_map/all_gather | solution.py:369
  11.2 1.0 copy-start.2
  29.2 671.7 %all-reduce.8.cloned.1.call-start = ((), (), s32[]{:S(2)}) async-start(), calls=%async_computation.2 | async-start | bytes 20971520 | tf_op jit(solution)/shard_map/psum | solution.py:458
  72.4 43.9 %copy-start.5 = (s32[32]{0:T(128)S(1)}, s32[32]{0:T(128)}, u32[]{:S(2)}) copy-start(s32[32]{0:T(128)} %param.10) | copy-start | bytes 388
  269.1 25.0 %copy-start.6 = (bf16[32,128,1024]{2,1,0:T(8,128)(2,1)S(1)}, bf16[32,128,1024]{2,1,0:T(8,128)(2,1)}, u32[]{:S(2)}) copy-start(bf16[32,128,1024]{2,1,0:T(8,128)(2,1)} %get-tuple-element.30.refs_0_) | copy-start | bytes 25165828
  499.4 5.8 slice-start.4
  502.1 3.2 slice-start.5
  505.2 21.9 %copy-start.3 = (f32[128,128]{1,0:T(8,128)S(1)}, f32[128,128]{1,0:T(8,128)}, u32[]{:S(2)}) copy-start(f32[128,128]{1,0:T(8,128)} %get-tuple-element.60.cos_ref.refs_6_) | copy-start | bytes 196612
  505.2 21.9 %copy-start.4 = (f32[128,128]{1,0:T(8,128)S(1)}, f32[128,128]{1,0:T(8,128)}, u32[]{:S(2)}) copy-start(f32[128,128]{1,0:T(8,128)} %get-tuple-element.61.sin_ref.refs_7_) | copy-start | bytes 196612
  527.2 27.8 %slice-start = ((s8[16777216]{0:T(1024)(128)(4,1)}), s8[4194304]{0:T(1024)(128)(4,1)S(1)}, s32[]{:S(2)}) async-start(s8[16777216]{0:T(1024)(128)(4,1)} %bitcast.27), calls=%async_computation.4 | async-start | bytes 8388608
  530.3 24.7 %copy-start = (bf16[32,128,128]{2,1,0:T(8,128)(2,1)}, bf16[32,128,128]{2,1,0:T(8,128)(2,1)S(1)}, u32[]{:S(2)}) copy-start(bf16[32,128,128]{2,1,0:T(8,128)(2,1)S(1)} %fusion.2) | copy-start | bytes 3145732
  530.3 24.7 %slice-start.1 = ((s8[16777216]{0:T(1024)(128)(4,1)}), s8[4194304]{0:T(1024)(128)(4,1)S(1)}, s32[]{:S(2)}) async-start(s8[16777216]{0:T(1024)(128)(4,1)} %bitcast.27), calls=%async_computation.5 | async-start | bytes 8388608
  530.3 24.7 %slice-start.2 = ((s8[16777216]{0:T(1024)(128)(4,1)}), s8[4194304]{0:T(1024)(128)(4,1)S(1)}, s32[]{:S(2)}) async-start(s8[16777216]{0:T(1024)(128)(4,1)} %bitcast.27), calls=%async_computation.6 | async-start | bytes 8388608
  530.3 24.7 %slice-start.3 = ((s8[16777216]{0:T(1024)(128)(4,1)}), s8[4194304]{0:T(1024)(128)(4,1)S(1)}, s32[]{:S(2)}) async-start(s8[16777216]{0:T(1024)(128)(4,1)} %bitcast.27), calls=%async_computation.7 | async-start | bytes 8388608
  561.6 1.2 copy-start.1
  561.6 350.0 %all-reduce.10.cloned.1.call-start = ((), (), s32[]{:S(2)}) async-start(), calls=%async_computation.3 | async-start | bytes 33554432 | tf_op jit(solution)/shard_map/psum | solution.py:446
  562.4 467.7 %all-reduce.6.cloned.1.call-start = ((), (), s32[]{:S(2)}) async-start(), calls=%async_computation | async-start | bytes 16777216 | tf_op jit(solution)/shard_map/psum | solution.py:449
Sparse Core Ops, SparseCore 0:
  29.3 86.9 all-gather.2
  561.7 139.0 all-reduce.7
  704.8 206.7 all-reduce.9
  914.9 115.0 all-reduce.5

commit v4 on v3

--- a/solution.py
+++ b/solution.py
@@ -14,8 +14,8 @@
 F32 = jnp.float32
 BF16 = jnp.bfloat16
 MESH = pl.DeviceIdType.MESH
-CHUNKS = 2
-SUBS = 2
+SUBS = (1, 3)
+CHUNKS = len(SUBS)
 SLOTS = 3
 LAG = 3
 VMEM_LIMIT = 60 * 1024 * 1024
@@ -65,7 +65,7 @@
             q_ref[:, :, lo:lo + hd] = rot.astype(BF16).reshape(nb, seq, hd)
 
 
-def attention_kernel(batch, first, last, *refs, scale):
+def attention_kernel(batch, subs, first, last, *refs, scale):
     refs = list(refs)
     prefix_ref, q_ref, do_ref, q_was, do_was, kv_ref, cos_ref, sin_ref = refs[:8]
     del refs[:8]
@@ -76,7 +76,7 @@
         (part, recv1, sum1, recv2, sum2, recv3,
          send1, got1, send2, got2, send3, got3, free1, free2, free3) = refs[13:]
     t = pl.program_id(0)
-    steps = SUBS * batch
+    steps = subs * batch
     me = lax.axis_index('sp')
     core = me % 2
     x_bit = (me // 2) % 2
@@ -131,9 +131,9 @@
 
     low = functools.partial(jnp.full, (8, 2 * hd), MASK_FILL, F32)
 
-    acc = part.at[((t + SUBS - 1) // SUBS + SLOTS - 1) % SLOTS] if last else dkv_ref.at[0]
-
-    @pl.when((t % SUBS == 1 % SUBS) & (t <= steps))
+    acc = part.at[((t + subs - 1) // subs + SLOTS - 1) % SLOTS] if last else dkv_ref.at[0]
+
+    @pl.when((t % subs == 1 % subs) & (t <= steps))
     def _():
         acc[...] = jnp.zeros(acc.shape, F32) if first else carry_ref[0]
 
@@ -218,8 +218,8 @@
 
     def stage(number):
         ahead = t - LAG * number
-        b = ahead // SUBS - 1
-        return b, (ahead >= SUBS) & (ahead % SUBS == 0) & (b < batch)
+        b = ahead // subs - 1
+        return b, (ahead >= subs) & (ahead % subs == 0) & (b < batch)
 
     b4, due4 = stage(3)
 
@@ -382,22 +382,23 @@
 
         f32_tile = (seq, hd)
         prefix = jnp.broadcast_to(prefix_len[:, None, None], (batch, 8, hd))
-        cols = width // CHUNKS
+        wide = width // sum(SUBS)
         split = (2, groups // 2, 2) + f32_tile
 
         def attend(n, q, d_o, carry):
             first, last = n == 0, n == CHUNKS - 1
-            top = SUBS * batch - 1
+            subs, skip = SUBS[n], sum(SUBS[:n])
+            cols = subs * wide
+            top = subs * batch - 1
             now = lambda i: jnp.minimum(i, top)
             before = lambda i: jnp.clip(i - 1, 0, top)
-            wide = cols // SUBS
-            here = lambda i: (before(i) // SUBS, 0, before(i) % SUBS)
-            part_spec = pl.BlockSpec((1,) + split, lambda i: (before(i) // SUBS, 0, 0, 0, 0, 0))
-            at_now = pl.BlockSpec((1, seq, wide), lambda i: (now(i) // SUBS, 0, SUBS * n + now(i) % SUBS))
-            at_before = pl.BlockSpec((1, seq, wide), lambda i: (before(i) // SUBS, 0, SUBS * n + before(i) % SUBS))
-            in_specs = [pl.BlockSpec((1, 8, hd), lambda i: (now(i) // SUBS, 0, 0)),
+            here = lambda i: (before(i) // subs, 0, before(i) % subs)
+            part_spec = pl.BlockSpec((1,) + split, lambda i: (before(i) // subs, 0, 0, 0, 0, 0))
+            at_now = pl.BlockSpec((1, seq, wide), lambda i: (now(i) // subs, 0, skip + now(i) % subs))
+            at_before = pl.BlockSpec((1, seq, wide), lambda i: (before(i) // subs, 0, skip + before(i) % subs))
+            in_specs = [pl.BlockSpec((1, 8, hd), lambda i: (now(i) // subs, 0, 0)),
                         at_now, at_now, at_before, at_before,
-                        pl.BlockSpec((groups, 1, seq, 2 * hd), lambda i: (0, now(i) // SUBS, 0, 0)),
+                        pl.BlockSpec((groups, 1, seq, 2 * hd), lambda i: (0, now(i) // subs, 0, 0)),
                         full(seq, hd), full(seq, hd)]
             args = [prefix, q, d_o, q, d_o, kv_all, cos2, sin2]
             if not first:
@@ -410,7 +411,7 @@
                 pltpu.VMEM((seq, seq), BF16), pltpu.VMEM((2, 8, 2 * hd), F32), pltpu.VMEM((2, 8, 2 * hd), F32)]
             params = dict(vmem_limit_bytes=VMEM_LIMIT)
             if last:
-                dkv_spec = pl.BlockSpec((1, seq, 2 * hd), lambda i: (jnp.maximum(i - SUBS - 3 * LAG, 0) // SUBS, 0, 0))
+                dkv_spec = pl.BlockSpec((1, seq, 2 * hd), lambda i: (jnp.maximum(i - subs - 3 * LAG, 0) // subs, 0, 0))
                 dkv_shape = jax.ShapeDtypeStruct((batch, seq, 2 * hd), F32)
                 scratch += [pltpu.VMEM((SLOTS,) + shape + f32_tile, F32) for shape in
                             ((2, groups // 2, 2), (4, 2), (2, 2, 2), (2, 2), (2, 2), (2,))]
@@ -420,8 +421,8 @@
                 dkv_spec = part_spec
                 dkv_shape = jax.ShapeDtypeStruct((batch,) + split, F32)
             return pl.pallas_call(
-                functools.partial(attention_kernel, batch, first, last, scale=scale),
-                grid=(SUBS * batch + 1 + 3 * LAG * last,),
+                functools.partial(attention_kernel, batch, subs, first, last, scale=scale),
+                grid=(subs * batch + 1 + 3 * LAG * last,),
                 in_specs=in_specs,
                 out_specs=[pl.BlockSpec((1, seq, wide), here), pl.BlockSpec((1, seq, wide), here), dkv_spec],
                 out_shape=[jax.ShapeDtypeStruct((batch, seq, cols), BF16),
@@ -465,7 +466,7 @@
         dx, dgain = pl.pallas_call(
             post_kernel,
             grid=(batch // nb2,),
-            in_specs=[rows_spec(nb2, cols)] * CHUNKS + [
+            in_specs=[rows_spec(nb2, c * wide) for c in SUBS] + [
                 rows_spec(nb2, 2 * hd), full(d_model, width), full(d_model, 2 * hd),
                 rows_spec(nb2, d_model), rows_spec(nb2, d_model), full(1, d_model)],
             out_specs=[rows_spec(nb2, d_model), full(8, d_model)],
@@ -479,7 +480,7 @@
         y = pl.pallas_call(
             out_kernel,
             grid=(batch // nb,),
-            in_specs=[rows_spec(nb, cols)] * CHUNKS + [full(width, d_model), rows_spec(nb, d_model)],
+            in_specs=[rows_spec(nb, c * wide) for c in SUBS] + [full(width, d_model), rows_spec(nb, d_model)],
             out_specs=rows_spec(nb, d_model),
             out_shape=jax.ShapeDtypeStruct((batch, seq, d_model), BF16),
             compiler_params=pltpu.CompilerParams(vmem_limit_bytes=VMEM_LIMIT),

time: 1060 us -> 938 us (0.88)
  waiting for transfers between devices: 322 us -> 162 us
  Pallas kernels: 502 us -> 542 us
    psum x1, waiting for transfers between devices: 208 us -> 0.01 us  [local_block(): lax.psum((d_wo, d_wq), 'sp', axis_index_groups=[[m ^ 1 for m in range(gro...]
    psum x1, waiting for transfers between devices: 5.39 us -> 160 us  [local_block(): d_wq, d_wkv = lax.psum((d_wq, d_wkv), 'sp')]
    psum x1, waiting for transfers between devices: 106 us -> 0.01 us  [local_block(): lax.psum(d_wo, 'sp', axis_index_groups=[[m ^ 2 for m in range(groups)]])]
    pallas_call x2, Pallas kernels: 336 us -> 376 us  [attend(): pl.pallas_call(functools.partial(attention_kernel, batch, subs, first, la...]
  transfers between devices with their start and end apart: 4 -> 4, of which waited for: 4 -> 2; matrix products, arithmetic and copies ran while one was open for 6% -> 15% of each run, Pallas kernels for 14% -> 49%
where the time goes in v4:
time: 938 us; the launch traced here: 929 us
  Pallas kernels  542 us (58%)
  waiting for transfers between devices  162 us (17%)
  matrix products  147 us (16%)
  other arithmetic  32.1 us (3%)
  blocking collectives  24.2 us (3%)
  between operations  14.4 us (2%)
    pallas_call x2, Pallas kernels, attend(): pl.pallas_call(functools.partial(attention_kernel, batch, subs, first, la...  376 us
    psum x1, waiting for transfers between devices, local_block(): d_wq, d_wkv = lax.psum((d_wq, d_wkv), 'sp')  160 us
    pallas_call x1, Pallas kernels, local_block(): pl.pallas_call(post_kernel, grid=(batch // nb2,), in_specs=[rows_spec(nb2...  62.5 us
    dot_general x2, matrix products, local_block(): d_wo = jnp.einsum('bse,bsd->ed', o, dy, preferred_element_type=F32)  49.9 us
    dot_general x2, matrix products, local_block(): d_wq = jnp.einsum('bsd,bse->de', xn, dq, preferred_element_type=F32)  44.9 us
    pallas_call x1, Pallas kernels, local_block(): pl.pallas_call(out_kernel, grid=(batch // nb,), in_specs=[rows_spec(nb, c...  43.3 us
    pallas_call x1, Pallas kernels, local_block(): pl.pallas_call(functools.partial(query_kernel, scale=scale), grid=(batch...  43.2 us
    dot_general x1, matrix products, local_block(): jnp.einsum('bsd,ed->bse', dy, w_o, preferred_element_type=F32).astype(BF16)  41.8 us
  transfers between devices with their start and end apart: 4, of which 2 were waited for; matrix products, arithmetic and copies ran while one was open for 15% of the time, Pallas kernels for 49%

profile of v4, /device:TPU:0, one launch (start us, length us, event | category | flops | bytes accessed | tf_op | source)
XLA Modules:
  0.0 928.9 jit_solution(506758903379858366)
XLA Ops:
  7.2 1.3 reshape.34
  8.5 1.1 constant_dynamic-update-slice_fusion.1
  10.0 1.2 constant_dynamic-update-slice_fusion.wkv_ref.refs_4_
  11.2 0.9 pad_maximum_fusion.3
  12.2 17.0 %norm.1 = (bf16[32,128,2048]{2,1,0:T(8,128)(2,1)}, bf16[32,128,256]{2,1,0:T(8,128)(2,1)}) custom-call(bf16[32,128,2048]{2,1,0:T(8,128)(2,1)} %refs_5_, f32[1,2048]{1,0:T(1,128)} %bitcast.25, bf16[2048,256]{1,0:T(8,128)(2,1)} %copy-done, f32[128,128]{1,0:T(8,128)} %get-tuple-element.60.cos_ref.refs_6_, f32[128,128]{1,0:T(8,128)} %get-tuple-element.61.sin_ref.refs_7_), custom_call_target="tpu_custom_call" | custom-call | flops 4294967296 | bytes 33554432 | tf_op jit(solution)/shard_map/norm/pallas_call | solution.py:357
  29.2 43.2 %query.1.refs_1_.refs_3_ = bf16[32,128,2048]{2,1,0:T(8,128)(2,1)} custom-call(bf16[32,128,2048]{2,1,0:T(8,128)(2,1)} %get-tuple-element.35.xn_ref, bf16[2048,2048]{1,0:T(8,128)(2,1)} %refs_3_.2, f32[128,128]{1,0:T(8,128)} %get-tuple-element.60.cos_ref.refs_6_, f32[128,128]{1,0:T(8,128)} %get-tuple-element.61.sin_ref.refs_7_), custom_call_target="tpu_custom_call" | custom-call | flops 34359738368 | bytes 33554432 | tf_op jit(solution)/shard_map/query/pallas_call | solution.py:370
  72.5 41.8 %convolution_convert_fusion.refs_2_.refs_4_ = bf16[32,128,2048]{2,1,0:T(8,128)(2,1)} fusion(bf16[32,128,2048]{2,1,0:T(8,128)(2,1)} %refs_6_, bf16[2048,2048]{1,0:T(8,128)(2,1)} %refs_2_.1), kind=kOutput, calls=%fused_computation.2 | convolution fusion | flops 34368126976 | bytes 41943040 | tf_op jit(solution)/shard_map/bsd,ed->bse/dot_general | solution.py:381
  114.3 2.1 all-gather.3.cloned.1.call-done
  117.1 74.3 %attend.2 = (bf16[32,128,512]{2,1,0:T(8,128)(2,1)}, bf16[32,128,512]{2,1,0:T(8,128)(2,1)}, f32[32,2,4,2,128,128]{5,4,3,2,1,0:T(8,128)}) custom-call(s32[32,8,128]{2,1,0:T(8,128)} %broadcast_in_dim.2.refs_0_, bf16[32,128,2048]{2,1,0:T(8,128)(2,1)} %query.1.refs_1_.refs_3_, bf16[32,128,2048]{2,1,0:T(8,128)(2,1)} %convolution_convert_fusion.refs_2_.refs_4_, ...), custom_call_target="tpu_custom_call" | custom-call | flops 25769803776 | bytes 25165824 | tf_op jit(solution)/shard_map/attend/pallas_call | solution.py:423
  191.4 15.3 %convolution_bitcast_fusion.3 = f32[512,2048]{1,0:T(8,128)} fusion(bf16[32,128,512]{2,1,0:T(8,128)(2,1)} %get-tuple-element.29.refs_0_, bf16[32,128,2048]{2,1,0:T(8,128)(2,1)} %refs_6_), kind=kOutput, calls=%fused_computation.7 | convolution fusion | flops 8589934592 | bytes 25165824 | tf_op jit(solution)/shard_map/bse,bsd->ed/dot_general | solution.py:443
  206.7 13.8 %convolution_bitcast_fusion.2 = f32[2048,512]{1,0:T(8,128)} fusion(bf16[32,128,2048]{2,1,0:T(8,128)(2,1)} %get-tuple-element.35.xn_ref, bf16[32,128,512]{2,1,0:T(8,128)(2,1)S(1)} %copy-done.4), kind=kOutput, calls=%fused_computation.6 | convolution fusion | flops 8589934592 | bytes 25165824 | tf_op jit(solution)/shard_map/bsd,bse->de/dot_general | solution.py:445
  220.6 301.5 %attend.3 = (bf16[32,128,1536]{2,1,0:T(8,128)(2,1)}, bf16[32,128,1536]{2,1,0:T(8,128)(2,1)}, f32[32,128,256]{2,1,0:T(8,128)}) custom-call(s32[32,8,128]{2,1,0:T(8,128)} %broadcast_in_dim.2.refs_0_, bf16[32,128,2048]{2,1,0:T(8,128)(2,1)} %query.1.refs_1_.refs_3_, bf16[32,128,2048]{2,1,0:T(8,128)(2,1)} %convolution_convert_fusion.refs_2_.refs_4_, ...), custom_call_target="tpu_custom_call" | custom-call | flops 77309411328 | bytes 75497472 | tf_op jit(solution)/shard_map/attend/pallas_call | solution.py:423
  522.1 34.6 %convolution_bitcast_fusion.1 = f32[1536,2048]{1,0:T(8,128)} fusion(bf16[32,128,1536]{2,1,0:T(8,128)(2,1)} %get-tuple-element.34.refs_1_, bf16[32,128,2048]{2,1,0:T(8,128)(2,1)} %refs_6_), kind=kOutput, calls=%fused_computation.4 | convolution fusion | flops 25769803776 | bytes 41943040 | tf_op jit(solution)/shard_map/bse,bsd->ed/dot_general | solution.py:443
  556.8 2.5 convert.5
  561.2 10.6 %convolution_bitcast_fusion.4 = f32[2048,256]{1,0:T(8,128)} fusion(bf16[32,128,2048]{2,1,0:T(8,128)(2,1)} %get-tuple-element.35.xn_ref, bf16[32,128,128]{2,1,0:T(8,128)(2,1)S(1)} %get-tuple-element.56, bf16[32,128,128]{2,1,0:T(8,128)(2,1)S(1)} %fusion.2), kind=kOutput, calls=%fused_computation.8 | convolution fusion | flops 4299161600 | bytes 20971520 | tf_op jit(solution)/shard_map/bsd,bse->de/dot_general | solution.py:457
  572.0 31.0 %convolution_bitcast_fusion = f32[2048,1536]{1,0:T(8,128)} fusion(bf16[32,128,2048]{2,1,0:T(8,128)(2,1)S(1)} %bitcast.28, bf16[32,128,1536]{2,1,0:T(8,128)(2,1)} %get-tuple-element.36.refs_1_), kind=kOutput, calls=%fused_computation.3 | convolution fusion | flops 25769803776 | bytes 41943040 | tf_op jit(solution)/shard_map/bsd,bse->de/dot_general | solution.py:451
  603.0 1.6 pad_maximum_fusion.2.refs_2_
  604.7 62.5 %norm_grad.1 = (bf16[32,128,2048]{2,1,0:T(8,128)(2,1)}, f32[8,2048]{1,0:T(8,128)}) custom-call(bf16[32,128,512]{2,1,0:T(8,128)(2,1)} %get-tuple-element.30.refs_0_, bf16[32,128,1536]{2,1,0:T(8,128)(2,1)} %get-tuple-element.36.refs_1_, bf16[32,128,256]{2,1,0:T(8,128)(2,1)} %pad_maximum_fusion.2.refs_2_, bf16[2048,2048]{1,0:T(8,128)(2,1)} %refs_3_.2, ...), custom_call_target="tpu_custom_call" | custom-call | flops 38654705664 | bytes 67108864 | tf_op jit(solution)/shard_map/norm_grad/pallas_call | solution.py:466
  668.0 24.2 %psum.47 = f32[2048]{0:T(1024)} all-reduce(f32[2048]{0:T(1024)S(1)} %reduce_sum.9), channel_id=1, replica_groups=mesh['sp'=8] {'sp'}, use_global_device_ids=true, to_apply=%region_6.0 | all-reduce | flops 2048 | bytes 16384 | tf_op jit(solution)/shard_map/psum | solution.py:479
  692.2 43.3 %output.1 = bf16[32,128,2048]{2,1,0:T(8,128)(2,1)} custom-call(bf16[32,128,512]{2,1,0:T(8,128)(2,1)} %get-tuple-element.29.refs_0_, bf16[32,128,1536]{2,1,0:T(8,128)(2,1)} %get-tuple-element.34.refs_1_, bf16[2048,2048]{1,0:T(8,128)(2,1)} %refs_2_.1, bf16[32,128,2048]{2,1,0:T(8,128)(2,1)} %refs_5_), custom_call_target="tpu_custom_call" | custom-call | flops 34359738368 | bytes 50331648 | tf_op jit(solution)/shard_map/output/pallas_call | solution.py:480
  735.6 11.8 %pad_maximum_fusion.1 = f32[2048,2048]{1,0:T(8,128)} fusion(f32[1536,2048]{1,0:T(8,128)} %all-reduce.6.cloned.1.call-done, f32[512,2048]{1,0:T(8,128)} %get-tuple-element.50), kind=kLoop, calls=%fused_computation.1 | loop fusion | flops 4194304 | bytes 33554432 | tf_op jit(solution)/shard_map/concatenate | solution.py:462
  747.4 159.8 %all-reduce.8.cloned.1.call-done = (f32[2048,1536]{1,0:T(8,128)}, f32[2048,256]{1,0:T(8,128)}) async-done(((f32[2048,1536]{1,0:T(8,128)}, f32[2048,256]{1,0:T(8,128)}), (f32[2048,1536]{1,0:T(8,128)}, f32[2048,256]{1,0:T(8,128)})) %all-reduce.8.cloned.1.call-update) | async-done | bytes 14680080 | tf_op jit(solution)/shard_map/psum | solution.py:459
  907.2 3.0 fusion.4
  910.2 11.7 %pad_maximum_fusion = f32[2048,2048]{1,0:T(8,128)} fusion(f32[2048,1536]{1,0:T(8,128)} %get-tuple-element.47, f32[2048,512]{1,0:T(8,128)} %get-tuple-element.49), kind=kLoop, calls=%fused_computation | loop fusion | flops 4194304 | bytes 33554432 | tf_op jit(solution)/shard_map/concatenate | solution.py:463
  (37 shorter events, 4.3 us)
Async XLA Ops:
  7.2 109.1 %all-gather.3.cloned.1.call-start = ((), (), s32[]{:S(2)}) async-start(), calls=%async_computation.1 | async-start | bytes 18874368 | tf_op jit(solution)/shard_map/all_gather | solution.py:369
  11.2 1.0 copy-start
  29.2 706.4 %all-reduce.10.cloned.1.call-start = ((), (), s32[]{:S(2)}) async-start(), calls=%async_computation.3 | async-start | bytes 16777216 | tf_op jit(solution)/shard_map/psum | solution.py:447
  72.5 43.9 %copy-start.3 = (s32[32]{0:T(128)S(1)}, s32[32]{0:T(128)}, u32[]{:S(2)}) copy-start(s32[32]{0:T(128)} %param.10) | copy-start | bytes 388
  191.4 15.3 %copy-start.4 = (bf16[32,128,512]{2,1,0:T(8,128)(2,1)S(1)}, bf16[32,128,512]{2,1,0:T(8,128)(2,1)}, u32[]{:S(2)}) copy-start(bf16[32,128,512]{2,1,0:T(8,128)(2,1)} %get-tuple-element.30.refs_0_) | copy-start | bytes 12582916
  220.5 515.0 %all-reduce.6.cloned.1.call-start = ((), (), s32[]{:S(2)}) async-start(), calls=%async_computation | async-start | bytes 25165824 | tf_op jit(solution)/shard_map/psum | solution.py:450
  556.7 350.4 %all-reduce.8.cloned.1.call-start = ((), (), s32[]{:S(2)}) async-start(), calls=%async_computation.2 | async-start | bytes 29360128 | tf_op jit(solution)/shard_map/psum | solution.py:459
  559.3 1.2 copy-start.1
  559.3 1.2 copy-start.2
  560.5 11.4 %slice-start = ((s8[16777216]{0:T(1024)(128)(4,1)}), s8[4194304]{0:T(1024)(128)(4,1)S(1)}, s32[]{:S(2)}) async-start(s8[16777216]{0:T(1024)(128)(4,1)} %bitcast.27), calls=%async_computation.4 | async-start | bytes 8388608
  561.2 10.7 %slice-start.1 = ((s8[16777216]{0:T(1024)(128)(4,1)}), s8[4194304]{0:T(1024)(128)(4,1)S(1)}, s32[]{:S(2)}) async-start(s8[16777216]{0:T(1024)(128)(4,1)} %bitcast.27), calls=%async_computation.5 | async-start | bytes 8388608
  561.2 10.7 %slice-start.2 = ((s8[16777216]{0:T(1024)(128)(4,1)}), s8[4194304]{0:T(1024)(128)(4,1)S(1)}, s32[]{:S(2)}) async-start(s8[16777216]{0:T(1024)(128)(4,1)} %bitcast.27), calls=%async_computation.6 | async-start | bytes 8388608
  561.2 10.8 %slice-start.3 = ((s8[16777216]{0:T(1024)(128)(4,1)}), s8[4194304]{0:T(1024)(128)(4,1)S(1)}, s32[]{:S(2)}) async-start(s8[16777216]{0:T(1024)(128)(4,1)} %bitcast.27), calls=%async_computation.7 | async-start | bytes 8388608
Sparse Core Ops, SparseCore 0:
  29.3 86.9 all-gather.2
  220.6 156.5 all-reduce.9
  556.9 162.3 all-reduce.5
  723.3 183.8 all-reduce.7
